TPU v7x, 128 devices: a whole 4x4x4 slice. The times are simulated.
128 devices in a mesh: fsdp: 128 (over z, y, x, core).
Axes of the slice: x: 4, y: 4, z: 4, core: 2. Of those that a mesh axis runs over, the one named last changes fastest.
Arguments:
- tok_ids: int32 [524288], P('fsdp')
- tok_labels: int32 [524288], P('fsdp')
- loss_mask: int32 [524288], P('fsdp')
- emb_table: bfloat16 [2048, 256], P('fsdp')
- gain_mlp: float32 [256], replicated
- gain_head: float32 [256], replicated
- w_gate: bfloat16 [256, 768], P('fsdp')
- w_up: bfloat16 [256, 768], P('fsdp')
- w_down: bfloat16 [768, 256], P('fsdp')
Outputs:
- output 1: float32 [], replicated
- output 2: float32 [2048, 256], P('fsdp')
- output 3: float32 [256, 768], P('fsdp')
- output 4: float32 [256, 768], P('fsdp')
- output 5: float32 [768, 256], P('fsdp')
All inputs are finite; a program needn't handle non-finite values.
Results may differ from a plain program's by a relative error of at most 0.00844.
Values are sent between devices in bfloat16 or wider.
A program may use at most 1 GiB of HBM per device.

v0:
```python
import jax
import jax.numpy as jnp
from jax import lax
from jax.sharding import PartitionSpec as P

NORM_EPS = 1e-6
ROW_CONTRACT = (((1,), (1,)), ((), ()))
TOK_CONTRACT = (((0,), (0,)), ((), ()))


def rms_scale(rows_wide, norm_gain):
    inv_rms = lax.rsqrt(jnp.mean(rows_wide * rows_wide, axis=-1, keepdims=True) + NORM_EPS)
    return (rows_wide * inv_rms * norm_gain).astype(jnp.bfloat16), inv_rms


def rms_back(rows_wide, inv_rms, norm_gain, grad_out):
    scaled_grad = grad_out * norm_gain
    return inv_rms * (scaled_grad - rows_wide * (inv_rms * inv_rms) * jnp.mean(scaled_grad * rows_wide, axis=-1, keepdims=True))


def mlp_forward(emb_rows, gain_mlp, gain_head, w_gate, w_up, w_down):
    emb_wide = emb_rows.astype(jnp.float32)
    a_norm, inv_first = rms_scale(emb_wide, gain_mlp)
    gate_wide = jnp.dot(a_norm, w_gate, preferred_element_type=jnp.float32).astype(jnp.bfloat16).astype(jnp.float32)
    up_wide = jnp.dot(a_norm, w_up, preferred_element_type=jnp.float32).astype(jnp.bfloat16).astype(jnp.float32)
    gate_sig = jax.nn.sigmoid(gate_wide)
    act_rows = (gate_wide * gate_sig * up_wide).astype(jnp.bfloat16)
    hid_wide = (emb_wide + jnp.dot(act_rows, w_down, preferred_element_type=jnp.float32)).astype(jnp.bfloat16).astype(jnp.float32)
    h_norm, inv_second = rms_scale(hid_wide, gain_head)
    return (emb_wide, inv_first, a_norm, gate_wide, up_wide, gate_sig, act_rows, hid_wide, inv_second), h_norm


def head_forward(h_norm, emb_table, tok_labels, tok_coef):
    logits = lax.dot_general(h_norm, emb_table, ROW_CONTRACT, preferred_element_type=jnp.float32)
    row_max = jnp.max(logits, axis=-1, keepdims=True)
    exp_rows = jnp.exp(logits - row_max)
    sum_exp = jnp.sum(exp_rows, axis=-1, keepdims=True)
    is_label = jnp.arange(logits.shape[1])[None, :] == tok_labels[:, None]
    picked = jnp.sum(jnp.where(is_label, logits, 0.0), axis=-1)
    tok_loss = row_max[:, 0] + jnp.log(sum_exp[:, 0]) - picked
    d_logits = ((exp_rows / sum_exp - is_label.astype(jnp.float32)) * tok_coef[:, None]).astype(jnp.bfloat16)
    return jnp.sum(tok_coef * tok_loss), d_logits


def mlp_backward(saved, d_hidden, gain_mlp, w_gate, w_up, w_down):
    emb_wide, inv_first, a_norm, gate_wide, up_wide, gate_sig, act_rows = saved[:7]
    hid_grad = d_hidden.astype(jnp.bfloat16)
    d_act = lax.dot_general(hid_grad, w_down, ROW_CONTRACT, preferred_element_type=jnp.float32)
    grad_down = lax.dot_general(act_rows, hid_grad, TOK_CONTRACT, preferred_element_type=jnp.float32)
    d_up = (d_act * gate_wide * gate_sig).astype(jnp.bfloat16)
    d_gate = (d_act * up_wide * gate_sig * (1.0 + gate_wide * (1.0 - gate_sig))).astype(jnp.bfloat16)
    grad_gate = lax.dot_general(a_norm, d_gate, TOK_CONTRACT, preferred_element_type=jnp.float32)
    grad_up = lax.dot_general(a_norm, d_up, TOK_CONTRACT, preferred_element_type=jnp.float32)
    d_anorm = lax.dot_general(d_gate, w_gate, ROW_CONTRACT, preferred_element_type=jnp.float32) + lax.dot_general(d_up, w_up, ROW_CONTRACT, preferred_element_type=jnp.float32)
    grad_x = d_hidden + rms_back(emb_wide, inv_first, gain_mlp, d_anorm)
    return grad_x, grad_gate, grad_up, grad_down


def solution(mesh):
    def gather_rows(row_shard):
        return lax.all_gather(row_shard, "fsdp", axis=0, tiled=True)

    def scatter_rows(full_rows):
        return lax.psum_scatter(full_rows, "fsdp", scatter_dimension=0, tiled=True)

    def device_step(tok_ids, tok_labels, loss_mask, table_shard, gain_mlp, gain_head, gate_shard, up_shard, down_shard):
        mask_wide = loss_mask.astype(jnp.float32)
        tok_coef = mask_wide / lax.psum(jnp.sum(mask_wide), "fsdp")
        table_full = gather_rows(table_shard)
        gate_full = gather_rows(gate_shard)
        up_full = gather_rows(up_shard)
        down_full = gather_rows(down_shard)
        emb_rows = jnp.take(table_full, tok_ids, axis=0)
        saved, h_norm = mlp_forward(emb_rows, gain_mlp, gain_head, gate_full, up_full, down_full)
        loss_part, d_logits = head_forward(h_norm, table_full, tok_labels, tok_coef)
        table_again, d_logits = lax.optimization_barrier((table_shard, d_logits))
        table_back = gather_rows(table_again)
        d_hnorm = jnp.dot(d_logits, table_back, preferred_element_type=jnp.float32)
        head_grad = lax.dot_general(d_logits, h_norm, TOK_CONTRACT, preferred_element_type=jnp.float32)
        d_hidden = rms_back(saved[7], saved[8], gain_head, d_hnorm)
        gate_again, up_again, down_again, d_hidden = lax.optimization_barrier((gate_shard, up_shard, down_shard, d_hidden))
        gate_back = gather_rows(gate_again)
        up_back = gather_rows(up_again)
        down_back = gather_rows(down_again)
        grad_x, grad_gate, grad_up, grad_down = mlp_backward(saved, d_hidden, gain_mlp, gate_back, up_back, down_back)
        grad_table = head_grad + jax.ops.segment_sum(grad_x, tok_ids, num_segments=table_back.shape[0])
        return (lax.psum(loss_part, "fsdp"), scatter_rows(grad_table), scatter_rows(grad_gate), scatter_rows(grad_up), scatter_rows(grad_down))

    row_spec = P("fsdp", None)
    tok_spec = P("fsdp")
    return jax.shard_map(device_step, mesh=mesh, in_specs=(tok_spec, tok_spec, tok_spec, row_spec, P(), P(), row_spec, row_spec, row_spec), out_specs=(P(), row_spec, row_spec, row_spec, row_spec), check_vma=False)
```

profile of v0, /device:TPU:0, one launch (start us, length us, event | category | flops | bytes accessed | tf_op | source)
XLA Modules:
  0.0 1273.7 jit_solution(11088513628241337421)
XLA Ops:
  9.3 68.4 %psum.14 = f32[]{:T(128)} all-reduce(f32[]{:T(128)} %convert_reduce_fusion), channel_id=1, replica_groups=mesh['fsdp'=128] {'fsdp'}, use_global_device_ids=true, to_apply=%region_1.0 | all-reduce | flops 1 | bytes 8 | tf_op jit(solution)/shard_map/psum | solution.py:68
  77.7 33.4 %all-gather = bf16[128,2,768]{2,1,0:T(2,128)(2,1)S(1)} all-gather(bf16[1,2,768]{2,1,0:T(2,128)(2,1)} %bitcast.24), channel_id=1, replica_groups=mesh['fsdp'=128] {'fsdp'}, dimensions={0}, use_global_device_ids=true | all-gather | bytes 396288 | tf_op jit(solution)/shard_map/all_gather | solution.py:61
  111.2 33.4 %all-gather.1 = bf16[128,2,768]{2,1,0:T(2,128)(2,1)S(1)} all-gather(bf16[1,2,768]{2,1,0:T(2,128)(2,1)} %bitcast.26), channel_id=1, replica_groups=mesh['fsdp'=128] {'fsdp'}, dimensions={0}, use_global_device_ids=true | all-gather | bytes 396288 | tf_op jit(solution)/shard_map/all_gather | solution.py:61
  144.8 33.8 %all-gather.2 = bf16[128,6,256]{2,1,0:T(8,128)(2,1)S(1)} all-gather(bf16[1,6,256]{2,1,0:T(8,128)(2,1)} %bitcast.22), channel_id=1, replica_groups=mesh['fsdp'=128] {'fsdp'}, dimensions={0}, use_global_device_ids=true | all-gather | bytes 396288 | tf_op jit(solution)/shard_map/all_gather | solution.py:61
  180.2 17.8 %gather_fusion = bf16[4096,256]{1,0:T(8,128)(2,1)} fusion(bf16[2048,256]{1,0:T(8,128)(2,1)} %all-gather.9.cloned.1.call-done, s32[4096]{0:T(1024)S(1)} %fusion.37), kind=kCustom, calls=%fused_computation | custom fusion | bytes 4210688 | tf_op jit(solution)/shard_map/jit(_take)/gather | solution.py:73
  204.3 6.2 fusion.2
  213.1 13.3 %fusion.46 = (f32[4096]{0:T(1024)S(1)}, f32[4096,2048]{0,1:T(8,128)}) fusion(bf16[2048,256]{1,0:T(8,128)(2,1)S(1)} %copy-done.2, bf16[4096,256]{0,1:T(8,128)(2,1)S(1)} %get-tuple-element.32, f32[256]{0:T(256)S(1)} %copy-done.15, f32[4096]{0:T(1024)S(1)} %get-tuple-element.28), kind=kOutput, calls=%fused_computation.77 | convolution fusion | flops 4307546112 | bytes 36733952 | tf_op jit(solution)/shard_map/dot_general | solution.py:34
  226.4 16.0 %fusion.1 = (f32[4096]{0:T(1024)S(1)}, f32[4096]{0:T(1024)S(1)}) fusion(f32[4096,2048]{0,1:T(8,128)} %get-tuple-element.34, f32[4096]{0:T(1024)S(1)} %get-tuple-element.33, s32[4096]{0:T(1024)S(1)} %copy-done.8), kind=kLoop, calls=%fused_computation.6 | loop fusion | flops 41934848 | bytes 33619968 | tf_op jit(solution)/shard_map/reduce_sum | solution.py:37
  246.7 12.2 multiply_convert_fusion
  259.0 8.9 fusion.33
  267.9 51.8 %all-gather.11.cloned.1.call-done = bf16[2048,256]{1,0:T(8,128)(2,1)} async-done(((bf16[16,256]{1,0:T(8,128)(2,1)}), bf16[2048,256]{1,0:T(8,128)(2,1)}) %all-gather.11.cloned.1.call-update) | async-done | bytes 1048592 | tf_op jit(solution)/shard_map/all_gather | solution.py:61
  319.7 11.9 fusion.20
  334.4 33.8 %all-gather.3 = bf16[128,6,256]{2,1,0:T(8,128)(2,1)S(1)} all-gather(bf16[1,6,256]{2,1,0:T(8,128)(2,1)S(1)} %bitcast.23), channel_id=1, replica_groups=mesh['fsdp'=128] {'fsdp'}, dimensions={0}, use_global_device_ids=true | all-gather | bytes 396288 | tf_op jit(solution)/shard_map/all_gather | solution.py:61
  368.4 33.7 %all-gather.4 = bf16[128,2,768]{2,1,0:T(2,128)(2,1)S(1)} all-gather(bf16[1,2,768]{2,1,0:T(2,128)(2,1)S(1)} %bitcast.25), channel_id=1, replica_groups=mesh['fsdp'=128] {'fsdp'}, dimensions={0}, use_global_device_ids=true | all-gather | bytes 396288 | tf_op jit(solution)/shard_map/all_gather | solution.py:61
  402.2 12.7 fusion.11
  421.6 33.4 %all-gather.5 = bf16[128,2,768]{2,1,0:T(2,128)(2,1)S(1)} all-gather(bf16[1,2,768]{2,1,0:T(2,128)(2,1)S(1)} %bitcast.27), channel_id=1, replica_groups=mesh['fsdp'=128] {'fsdp'}, dimensions={0}, use_global_device_ids=true | all-gather | bytes 396288 | tf_op jit(solution)/shard_map/all_gather | solution.py:61
  455.1 6.2 fusion.40
  461.3 8.6 fusion.28
  470.2 7.3 fusion.27
  483.2 23.6 %scatter_fusion = f32[2048,256]{1,0:T(8,128)S(1)} fusion(f32[2048,256]{1,0:T(8,128)S(1)} %fusion.33, s32[4096]{0:T(1024)S(1)} %copy-done.7, f32[4096,256]{1,0:T(8,128)} %copy.18), kind=kCustom, calls=%fused_computation.1 | custom fusion | flops 1048576 | bytes 12599296 | tf_op jit(solution)/shard_map/scatter-add | solution.py:86
  514.1 321.1 %fusion = f32[8,256]{1,0:T(8,128)S(1)} fusion(f32[768,256]{1,0:T(8,128)S(1)} %fusion.29), kind=kCustom, calls=%all-reduce-scatter | all-reduce-scatter fusion | flops 262145 | bytes 794624
  846.9 11.9 collective-permute-start.22
  917.3 65.2 %psum.15 = f32[]{:T(128)} all-reduce(f32[]{:T(128)} %get-tuple-element.21), channel_id=1, replica_groups=mesh['fsdp'=128] {'fsdp'}, use_global_device_ids=true, to_apply=%region_8.9 | all-reduce | flops 1 | bytes 8 | tf_op jit(solution)/shard_map/psum | solution.py:87
  987.4 279.3 %reduce-scatter.4.cloned.1.call-done = f32[16,256]{1,0:T(8,128)} async-done(((f32[2048,256]{1,0:T(8,128)}), f32[16,256]{1,0:T(8,128)}) %reduce-scatter.4.cloned.1.call-update) | async-done | bytes 16400 | tf_op jit(solution)/shard_map/reduce_scatter | solution.py:64
  (136 shorter events, 115.0 us)
Async XLA Ops:
  7.2 173.0 %all-gather.9.cloned.1.call-start = ((), (), s32[]{:S(2)}) async-start(), calls=%async_computation.1 | async-start | bytes 1056768 | tf_op jit(solution)/shard_map/all_gather | solution.py:61
  7.9 311.8 %all-gather.11.cloned.1.call-start = ((), (), s32[]{:S(2)}) async-start(), calls=%async_computation.2 | async-start | bytes 1056768 | tf_op jit(solution)/shard_map/all_gather | solution.py:61
  259.0 727.1 %all-reduce.7.cloned.1.call-start = ((), (), s32[]{:S(2)}) async-start(), calls=%async_computation.4 | async-start | bytes 3145728
  469.9 796.8 %reduce-scatter.4.cloned.1.call-start = ((), (), s32[]{:S(2)}) async-start(), calls=%async_computation.3 | async-start | bytes 2113536 | tf_op jit(solution)/shard_map/reduce_scatter | solution.py:64
  841.6 17.1 %collective-permute-start.26 = (f32[8,256]{1,0:T(8,128)S(1)}, f32[8,256]{1,0:T(8,128)S(1)}, u32[]{:S(2)}, u32[]{:S(2)}) collective-permute-start(f32[8,256]{1,0:T(8,128)S(1)} %fusion), channel_id=1, source_target_pairs={{0,27},{1,28},{2,29},{3,30},{4,31},{5,32},{6,33},{7,34},{8,35},{9,... | collective-permute-start | bytes 24584
  843.0 19.9 %collective-permute-start.25 = (f32[8,256]{1,0:T(8,128)S(1)}, f32[8,256]{1,0:T(8,128)S(1)}, u32[]{:S(2)}, u32[]{:S(2)}) collective-permute-start(f32[8,256]{1,0:T(8,128)S(1)} %fusion), channel_id=1, source_target_pairs={{0,26},{1,27},{2,28},{3,29},{4,30},{5,31},{6,32},{7,33},{8,34},{9,... | collective-permute-start | bytes 24584
  844.3 20.6 %collective-permute-start.24 = (f32[8,256]{1,0:T(8,128)S(1)}, f32[8,256]{1,0:T(8,128)S(1)}, u32[]{:S(2)}, u32[]{:S(2)}) collective-permute-start(f32[8,256]{1,0:T(8,128)S(1)} %fusion), channel_id=1, source_target_pairs={{0,25},{1,26},{2,27},{3,28},{4,29},{5,30},{6,31},{7,32},{8,33},{9,... | collective-permute-start | bytes 24584
  845.6 23.0 %collective-permute-start.23 = (f32[8,256]{1,0:T(8,128)S(1)}, f32[8,256]{1,0:T(8,128)S(1)}, u32[]{:S(2)}, u32[]{:S(2)}) collective-permute-start(f32[8,256]{1,0:T(8,128)S(1)} %fusion), channel_id=1, source_target_pairs={{0,24},{1,25},{2,26},{3,27},{4,28},{5,29},{6,30},{7,31},{8,32},{9,... | collective-permute-start | bytes 24584
  846.9 23.0 %collective-permute-start.22 = (f32[8,256]{1,0:T(8,128)S(1)}, f32[8,256]{1,0:T(8,128)S(1)}, u32[]{:S(2)}, u32[]{:S(2)}) collective-permute-start(f32[8,256]{1,0:T(8,128)S(1)} %fusion), channel_id=1, source_target_pairs={{0,23},{1,24},{2,25},{3,26},{4,27},{5,28},{6,29},{7,30},{8,31},{9,... | collective-permute-start | bytes 24584
  858.8 13.7 %collective-permute-start.21 = (f32[8,256]{1,0:T(8,128)S(1)}, f32[8,256]{1,0:T(8,128)S(1)}, u32[]{:S(2)}, u32[]{:S(2)}) collective-permute-start(f32[8,256]{1,0:T(8,128)S(1)} %fusion), channel_id=1, source_target_pairs={{0,22},{1,23},{2,24},{3,25},{4,26},{5,27},{6,28},{7,29},{8,30},{9,... | collective-permute-start | bytes 24584
  862.9 12.7 collective-permute-start.20
  875.5 14.2 %collective-permute-start.15 = (f32[8,256]{1,0:T(8,128)S(1)}, f32[8,256]{1,0:T(8,128)S(1)}, u32[]{:S(2)}, u32[]{:S(2)}) collective-permute-start(f32[8,256]{1,0:T(8,128)S(1)} %fusion), channel_id=1, source_target_pairs={{0,16},{1,17},{2,18},{3,19},{4,20},{5,21},{6,22},{7,23},{8,24},{9,... | collective-permute-start | bytes 24584
  876.9 14.2 %collective-permute-start.14 = (f32[8,256]{1,0:T(8,128)S(1)}, f32[8,256]{1,0:T(8,128)S(1)}, u32[]{:S(2)}, u32[]{:S(2)}) collective-permute-start(f32[8,256]{1,0:T(8,128)S(1)} %fusion), channel_id=1, source_target_pairs={{0,15},{1,16},{2,17},{3,18},{4,19},{5,20},{6,21},{7,22},{8,23},{9,... | collective-permute-start | bytes 24584
  878.8 13.6 %collective-permute-start.13 = (f32[8,256]{1,0:T(8,128)S(1)}, f32[8,256]{1,0:T(8,128)S(1)}, u32[]{:S(2)}, u32[]{:S(2)}) collective-permute-start(f32[8,256]{1,0:T(8,128)S(1)} %fusion), channel_id=1, source_target_pairs={{0,14},{1,15},{2,16},{3,17},{4,18},{5,19},{6,20},{7,21},{8,22},{9,... | collective-permute-start | bytes 24584
  881.7 13.5 %collective-permute-start.12 = (f32[8,256]{1,0:T(8,128)S(1)}, f32[8,256]{1,0:T(8,128)S(1)}, u32[]{:S(2)}, u32[]{:S(2)}) collective-permute-start(f32[8,256]{1,0:T(8,128)S(1)} %fusion), channel_id=1, source_target_pairs={{0,13},{1,14},{2,15},{3,16},{4,17},{5,18},{6,19},{7,20},{8,21},{9,... | collective-permute-start | bytes 24584
  892.3 13.2 %collective-permute-start.8 = (f32[8,256]{1,0:T(8,128)S(1)}, f32[8,256]{1,0:T(8,128)S(1)}, u32[]{:S(2)}, u32[]{:S(2)}) collective-permute-start(f32[8,256]{1,0:T(8,128)S(1)} %fusion), channel_id=1, source_target_pairs={{0,9},{1,10},{2,11},{3,12},{4,13},{5,14},{6,15},{7,16},{8,17},{9,1... | collective-permute-start | bytes 24584
  895.2 15.3 %collective-permute-start.7 = (f32[8,256]{1,0:T(8,128)S(1)}, f32[8,256]{1,0:T(8,128)S(1)}, u32[]{:S(2)}, u32[]{:S(2)}) collective-permute-start(f32[8,256]{1,0:T(8,128)S(1)} %fusion), channel_id=1, source_target_pairs={{0,8},{1,9},{2,10},{3,11},{4,12},{5,13},{6,14},{7,15},{8,16},{9,17... | collective-permute-start | bytes 24584
  897.4 14.4 %collective-permute-start.6 = (f32[8,256]{1,0:T(8,128)S(1)}, f32[8,256]{1,0:T(8,128)S(1)}, u32[]{:S(2)}, u32[]{:S(2)}) collective-permute-start(f32[8,256]{1,0:T(8,128)S(1)} %fusion), channel_id=1, source_target_pairs={{0,7},{1,8},{2,9},{3,10},{4,11},{5,12},{6,13},{7,14},{8,15},{9,16}... | collective-permute-start | bytes 24584
  901.8 13.1 %collective-permute-start.5 = (f32[8,256]{1,0:T(8,128)S(1)}, f32[8,256]{1,0:T(8,128)S(1)}, u32[]{:S(2)}, u32[]{:S(2)}) collective-permute-start(f32[8,256]{1,0:T(8,128)S(1)} %fusion), channel_id=1, source_target_pairs={{0,6},{1,7},{2,8},{3,9},{4,10},{5,11},{6,12},{7,13},{8,14},{9,15},... | collective-permute-start | bytes 24584
  903.4 79.1 %collective-permute-start.4 = (f32[8,256]{1,0:T(8,128)S(1)}, f32[8,256]{1,0:T(8,128)S(1)}, u32[]{:S(2)}, u32[]{:S(2)}) collective-permute-start(f32[8,256]{1,0:T(8,128)S(1)} %fusion), channel_id=1, source_target_pairs={{0,5},{1,6},{2,7},{3,8},{4,9},{5,10},{6,11},{7,12},{8,13},{9,14},{... | collective-permute-start | bytes 24584
  905.5 76.9 %collective-permute-start.3 = (f32[8,256]{1,0:T(8,128)S(1)}, f32[8,256]{1,0:T(8,128)S(1)}, u32[]{:S(2)}, u32[]{:S(2)}) collective-permute-start(f32[8,256]{1,0:T(8,128)S(1)} %fusion), channel_id=1, source_target_pairs={{0,4},{1,5},{2,6},{3,7},{4,8},{5,9},{6,10},{7,11},{8,12},{9,13},{1... | collective-permute-start | bytes 24584
  910.5 71.9 %collective-permute-start.2 = (f32[8,256]{1,0:T(8,128)S(1)}, f32[8,256]{1,0:T(8,128)S(1)}, u32[]{:S(2)}, u32[]{:S(2)}) collective-permute-start(f32[8,256]{1,0:T(8,128)S(1)} %fusion), channel_id=1, source_target_pairs={{0,3},{1,4},{2,5},{3,6},{4,7},{5,8},{6,9},{7,10},{8,11},{9,12},{10... | collective-permute-start | bytes 24584
  911.8 70.6 %collective-permute-start.1 = (f32[8,256]{1,0:T(8,128)S(1)}, f32[8,256]{1,0:T(8,128)S(1)}, u32[]{:S(2)}, u32[]{:S(2)}) collective-permute-start(f32[8,256]{1,0:T(8,128)S(1)} %fusion), channel_id=1, source_target_pairs={{0,2},{1,3},{2,4},{3,5},{4,6},{5,7},{6,8},{7,9},{8,10},{9,11},{10,... | collective-permute-start | bytes 24584
  914.9 67.6 %collective-permute-start = (f32[8,256]{1,0:T(8,128)S(1)}, f32[8,256]{1,0:T(8,128)S(1)}, u32[]{:S(2)}, u32[]{:S(2)}) collective-permute-start(f32[8,256]{1,0:T(8,128)S(1)} %fusion), channel_id=1, source_target_pairs={{0,1},{1,2},{2,3},{3,4},{4,5},{5,6},{6,7},{7,8},{8,9},{9,10},{10,1... | collective-permute-start | bytes 24584
  (30 other events, 290.5 us)
Sparse Core Ops, SparseCore 0:
  10.8 66.1 all-gather.8
  259.1 60.5 all-gather.10
  470.0 147.6 all-reduce.6
  620.5 646.1 reduce-scatter.3
where the time goes:
time: 1280 us; the launch traced here: 1270 us
  blocking collectives  656 us (51%)
  waiting for transfers between devices  332 us (26%)
  matrix products  84.6 us (7%)
  starting transfers between devices  82 us (6%)
  other arithmetic  68.1 us (5%)
  local copies, waits for them, and re-layouts  36.1 us (3%)
  between operations  14.9 us (1%)
    unnamed x1, blocking collectives  321 us
    reduce_scatter x1, waiting for transfers between devices, scatter_rows(): return lax.psum_scatter(full_rows, 'fsdp', scatter_dimension=0, tiled=True)  279 us
    all_gather x6, blocking collectives, gather_rows(): return lax.all_gather(row_shard, 'fsdp', axis=0, tiled=True)  201 us
    unnamed x33, starting transfers between devices  81.6 us
    psum x1, blocking collectives, device_step(): tok_coef = mask_wide / lax.psum(jnp.sum(mask_wide), 'fsdp')  68.4 us
    psum x1, blocking collectives, device_step(): lax.psum(loss_part, 'fsdp')  65.2 us
    all_gather x2, waiting for transfers between devices, gather_rows(): return lax.all_gather(row_shard, 'fsdp', axis=0, tiled=True)  51.8 us
  transfers between devices with their start and end apart: 36, of which 2 were waited for; matrix products, arithmetic and copies ran while one was open for 30% of the time, Pallas kernels for 0%

commit v1 on v0

v1 whole, which is shorter than its diff:
```python
import functools

import jax
import jax.numpy as jnp
from jax import lax
from jax.experimental import pallas as pl
from jax.experimental.pallas import tpu as pltpu
from jax.sharding import PartitionSpec as P

NORM_EPS = 1e-6
ROW_CONTRACT = (((1,), (1,)), ((), ()))
MESH = pl.DeviceIdType.MESH
AXIS = "fsdp"
STRIDES = (2, 8, 32)
N_STREAM = 6
AG_ROWS = 96
AG_GATE, AG_UP, AG_DOWN, AG_CNT = 32, 44, 56, 68
RS_ROWS = 72
RS_GATE, RS_UP, RS_DOWN, RS_LOSS = 32, 44, 56, 68
RS_STREAMS = ((0, 16), (16, 16), (32, 16), (48, 8), (56, 8), (64, 8))


def torus_partner(v, t):
    near = v + 1 - 2 * lax.rem(v, 2)
    far = 3 - v
    return near + t * (far - near)


def my_place():
    me = lax.axis_index(AXIS)
    core = lax.rem(me, 2)
    coords = (lax.rem(lax.div(me, 2), 4), lax.rem(lax.div(me, 8), 4), lax.div(me, 32))
    return me, core, coords


def greet(me, core, coords):
    barrier = pltpu.get_barrier_semaphore()
    pl.semaphore_signal(barrier, inc=1, device_id=(me + 1 - 2 * core,), device_id_type=MESH)
    for d in range(3):
        for t in range(2):
            other = me + (torus_partner(coords[d], t) - coords[d]) * STRIDES[d]
            pl.semaphore_signal(barrier, inc=1, device_id=(other,), device_id_type=MESH)
    return barrier


def link_of(k, s, core):
    return (k + s) % 3, lax.rem(core + ((k + s) // 3) % 2, 2)


def send_copy(src, dst, send_sem, recv_sem, target):
    return pltpu.make_async_remote_copy(src_ref=src, dst_ref=dst, send_sem=send_sem, recv_sem=recv_sem, device_id=(target,), device_id_type=MESH)


def gather_kernel(e_ref, wg_ref, wu_ref, wd_ref, mask_ref, out_ref, buf, pack, send_sem, recv_sem, side_send, side_recv, out_sem):
    me, core, coords = my_place()
    cx, cy, cz = coords
    barrier = greet(me, core, coords)
    wide = jnp.float32
    pack[0:16, :] = e_ref[:, 0:128].astype(wide)
    pack[16:32, :] = e_ref[:, 128:256].astype(wide)
    for base, ref in ((AG_GATE, wg_ref), (AG_UP, wu_ref), (AG_DOWN, wd_ref)):
        vals = ref[...].astype(wide)
        tiles = vals.shape[1] // 128
        for r in range(vals.shape[0]):
            for c in range(tiles):
                row = base + r * tiles + c
                pack[row:row + 1, :] = vals[r:r + 1, c * 128:(c + 1) * 128]
    pack[AG_CNT:AG_ROWS, :] = jnp.zeros((AG_ROWS - AG_CNT, 128), wide)
    pack[AG_CNT:AG_CNT + 1, :] = jnp.sum(mask_ref[...].astype(wide), axis=0, keepdims=True)
    buf[cz, cy, cx, core] = pack[...].astype(jnp.bfloat16)
    pl.semaphore_wait(barrier, 7)

    def pieces(k, s):
        held = []
        for d in range(3):
            done = [q for q in range(s) if (k + q) % 3 == d]
            v = coords[d]
            if not done:
                held.append([pl.ds(v, 1)])
            elif len(done) == 1:
                _, t = link_of(k, done[0], core)
                held.append([pl.ds(v, 1), pl.ds(torus_partner(v, t), 1)])
            else:
                held.append([pl.ds(0, 4)])
        return [(iz, iy, ix) for iz in held[2] for iy in held[1] for ix in held[0]]

    pending = {}
    for s in range(6):
        for k in range(N_STREAM):
            if s > 0:
                for c in pending[k, s - 1]:
                    c.wait_recv()
            d, t = link_of(k, s, core)
            target = me + (torus_partner(coords[d], t) - coords[d]) * STRIDES[d]
            base = sum(len(pending[k, q]) for q in range(s))
            copies = []
            for i, (iz, iy, ix) in enumerate(pieces(k, s)):
                ref = buf.at[iz, iy, ix, core, pl.ds(16 * k, 16), :]
                c = send_copy(ref, ref, send_sem.at[k, base + i], recv_sem.at[k, base + i], target)
                c.start()
                copies.append(c)
            pending[k, s] = copies
    last = []
    for k in range(N_STREAM):
        for c in pending[k, 5]:
            c.wait_recv()
        ref = buf.at[:, :, :, core, pl.ds(16 * k, 16), :]
        c = send_copy(ref, ref, side_send.at[k], side_recv.at[k], me + 1 - 2 * core)
        c.start()
        last.append(c)
    for c in last:
        c.wait_recv()
    out = pltpu.make_async_copy(buf, out_ref, out_sem)
    out.start()
    for copies in pending.values():
        for c in copies:
            c.wait_send()
    for c in last:
        c.wait_send()
    out.wait()


def gather_all(table_shard, gate_shard, up_shard, down_shard, mask):
    vm = pl.BlockSpec(memory_space=pltpu.VMEM)
    return pl.pallas_call(
        gather_kernel,
        out_shape=jax.ShapeDtypeStruct((4, 4, 4, 2, AG_ROWS, 128), jnp.bfloat16),
        in_specs=[vm] * 5,
        out_specs=pl.BlockSpec(memory_space=pl.ANY),
        scratch_shapes=[
            pltpu.VMEM((4, 4, 4, 2, AG_ROWS, 128), jnp.bfloat16),
            pltpu.VMEM((AG_ROWS, 128), jnp.float32),
            pltpu.SemaphoreType.DMA((N_STREAM, 21)),
            pltpu.SemaphoreType.DMA((N_STREAM, 21)),
            pltpu.SemaphoreType.DMA((N_STREAM,)),
            pltpu.SemaphoreType.DMA((N_STREAM,)),
            pltpu.SemaphoreType.DMA,
        ],
        compiler_params=pltpu.CompilerParams(collective_id=0, has_side_effects=True, vmem_limit_bytes=32 << 20),
        name="gather_all",
    )(table_shard, gate_shard, up_shard, down_shard, mask)


def recv_shape(k, s):
    sizes = [4, 4, 4]
    for q in range(s + 1):
        sizes[(k + q) % 3] //= 2
    return sizes[2], sizes[1], sizes[0]


def reduce_kernel(g_ref, *refs):
    loss_ref, e_out, wg_out, wu_out, wd_out = refs[:5]
    acc, side, res = refs[5:8]
    recv = refs[8:8 + 36]
    send_sem, recv_sem, side_send, side_recv, own_sem = refs[44:]
    me, core, coords = my_place()
    barrier = greet(me, core, coords)
    own = []
    for k, (r0, rn) in enumerate(RS_STREAMS):
        c = pltpu.make_async_copy(g_ref.at[:, :, :, core, pl.ds(r0, rn), :], acc.at[:, :, :, pl.ds(r0, rn), :], own_sem.at[k])
        c.start()
        own.append(c)
    pl.semaphore_wait(barrier, 7)
    sides = []
    for k, (r0, rn) in enumerate(RS_STREAMS):
        c = send_copy(g_ref.at[:, :, :, 1 - core, pl.ds(r0, rn), :], side.at[:, :, :, pl.ds(r0, rn), :], side_send.at[k], side_recv.at[k], me + 1 - 2 * core)
        c.start()
        sides.append(c)

    def at_dim(d, idx):
        full = [slice(None)] * 3
        full[2 - d] = idx
        return tuple(full)

    pending = {}
    for s in range(7):
        for k, (r0, rn) in enumerate(RS_STREAMS):
            rows = pl.ds(r0, rn)
            if s == 0:
                own[k].wait()
                sides[k].wait_recv()
                acc[:, :, :, rows, :] += side[:, :, :, rows, :]
                cur = acc.at[:, :, :, rows, :]
            else:
                q = s - 1
                for c in pending[k, q]:
                    c.wait_recv()
                d, t = link_of(k, q, core)
                v = coords[d]
                prev = acc.at[:, :, :, rows, :] if q == 0 else recv[k * 6 + q - 1]
                cur = recv[k * 6 + q]
                if q < 3:
                    mate = torus_partner(v, 1 - t)
                    lo = jnp.minimum(v, mate)
                    hi = jnp.maximum(v, mate)
                    for j, idx in enumerate((lo, hi)):
                        at = at_dim(d, pl.ds(j, 1))
                        cur[at] += prev[at_dim(d, pl.ds(idx, 1))]
                else:
                    mate = torus_partner(v, t)
                    keep = jnp.where(v > mate, 1, 0)
                    cur[...] += prev[at_dim(d, pl.ds(keep, 1))]
            if s == 6:
                res[rows, :] = cur[0, 0, 0]
                continue
            d, t = link_of(k, s, core)
            v = coords[d]
            mate = torus_partner(v, t)
            target = me + (mate - v) * STRIDES[d]
            dst = recv[k * 6 + s]
            copies = []
            if s < 3:
                far = torus_partner(mate, 1 - t)
                lo = jnp.minimum(mate, far)
                hi = jnp.maximum(mate, far)
                for j, idx in enumerate((lo, hi)):
                    c = send_copy(cur.at[at_dim(d, pl.ds(idx, 1))], dst.at[at_dim(d, pl.ds(j, 1))], send_sem.at[k, 2 * s + j], recv_sem.at[k, 2 * s + j], target)
                    c.start()
                    copies.append(c)
            else:
                give = jnp.where(v > mate, 0, 1)
                c = send_copy(cur.at[at_dim(d, pl.ds(give, 1))], dst, send_sem.at[k, 3 + s], recv_sem.at[k, 3 + s], target)
                c.start()
                copies.append(c)
            pending[k, s] = copies
    loss_ref[...] = res[RS_LOSS:RS_LOSS + 1, :]
    e_out[:, 0:128] = res[0:16, :]
    e_out[:, 128:256] = res[16:32, :]
    for base, ref in ((RS_GATE, wg_out), (RS_UP, wu_out), (RS_DOWN, wd_out)):
        tiles = ref.shape[1] // 128
        for r in range(ref.shape[0]):
            for c in range(tiles):
                row = base + r * tiles + c
                ref[r:r + 1, c * 128:(c + 1) * 128] = res[row:row + 1, :]
    for copies in pending.values():
        for c in copies:
            c.wait_send()
    for c in sides:
        c.wait_send()


def reduce_all(grads):
    vm = pl.BlockSpec(memory_space=pltpu.VMEM)
    sds = lambda *shape: jax.ShapeDtypeStruct(shape, jnp.float32)
    recvs = [pltpu.VMEM((*recv_shape(k, s), rn, 128), jnp.float32) for k, (_, rn) in enumerate(RS_STREAMS) for s in range(6)]
    return pl.pallas_call(
        reduce_kernel,
        out_shape=(sds(1, 128), sds(16, 256), sds(2, 768), sds(2, 768), sds(6, 256)),
        in_specs=[pl.BlockSpec(memory_space=pl.ANY)],
        out_specs=(vm,) * 5,
        scratch_shapes=[
            pltpu.VMEM((4, 4, 4, RS_ROWS, 128), jnp.float32),
            pltpu.VMEM((4, 4, 4, RS_ROWS, 128), jnp.float32),
            pltpu.VMEM((RS_ROWS, 128), jnp.float32),
            *recvs,
            pltpu.SemaphoreType.DMA((N_STREAM, 9)),
            pltpu.SemaphoreType.DMA((N_STREAM, 9)),
            pltpu.SemaphoreType.DMA((N_STREAM,)),
            pltpu.SemaphoreType.DMA((N_STREAM,)),
            pltpu.SemaphoreType.DMA((N_STREAM,)),
        ],
        compiler_params=pltpu.CompilerParams(collective_id=1, has_side_effects=True, vmem_limit_bytes=32 << 20),
        name="reduce_all",
    )(grads)


TILE = 512
N_TILE = 4096 // TILE
V_CHUNK = 512
F_CHUNK = 256


def mm(a, b):
    return jnp.dot(a, b, preferred_element_type=jnp.float32)


def mm_nt(a, b):
    return lax.dot_general(a, b, ROW_CONTRACT, preferred_element_type=jnp.float32)


def step_kernel(gath, ids, labels, mask, g1, g2, g_out, loss_out, e_s, et_s, wg_s, wgt_s, wu_s, wut_s, wd_s, wdt_s, g1_s, g2_s, d_e, d_wg, d_wu, d_wd, logit_s, dl_s, oh_s, sl_s, dp_s, u_s, dh_s, dq_s, dpb_s, stage):
    f32, bf16 = jnp.float32, jnp.bfloat16
    rows = g_out.reshape(128 * RS_ROWS, 128)
    g_out[:, 0:48, :] = gath[:, 32:80, :].astype(f32)
    for base, acc, w, wt in ((AG_GATE, d_wg, wg_s, wgt_s), (AG_UP, d_wu, wu_s, wut_s), (AG_DOWN, d_wd, wd_s, wdt_s)):
        n = acc.shape[0]
        per, tiles = n // 128, acc.shape[1] // 128
        for c in range(tiles):
            for r in range(per):
                stage[pl.ds(c * n + r, 128, stride=per), :] = rows[pl.ds(base - 32 + r * tiles + c, 128, stride=RS_ROWS), :]
            acc[:, c * 128:(c + 1) * 128] = stage[c * n:(c + 1) * n, :]
        w[...] = acc[...].astype(bf16)
        wt[...] = acc[...].T.astype(bf16)
        acc[...] = jnp.zeros_like(acc)
    total = jnp.sum(g_out[:, AG_CNT - 32, :])
    for half in range(2):
        part = gath[:, 16 * half:16 * half + 16, :].reshape(2048, 128)
        e_s[:, 128 * half:128 * half + 128] = part
        et_s[128 * half:128 * half + 128, :] = part.T
    g1_s[...] = jnp.broadcast_to(g1[...], (128, 256)).T
    g2_s[...] = jnp.broadcast_to(g2[...], (128, 256)).T
    d_e[...] = jnp.zeros_like(d_e)
    loss_out[...] = jnp.zeros_like(loss_out)

    def wide_gain(ref):
        return jnp.concatenate([ref[...]] * (TILE // 128), axis=1)

    def norm(x, gain):
        r = lax.rsqrt(jnp.mean(x * x, axis=0, keepdims=True) + NORM_EPS)
        return (x * r * gain).astype(bf16), r

    def norm_back(x, r, gain, grad):
        sg = grad * gain
        return r * (sg - x * (r * r) * jnp.mean(sg * x, axis=0, keepdims=True))

    def tile_step(i, carry):
        id_row, label_row = ids[i], labels[i]
        coef = mask[i].astype(f32) / total
        for v in range(0, 2048, V_CHUNK):
            vocab = lax.broadcasted_iota(jnp.int32, (V_CHUNK, TILE), 0) + v
            oh_s[v:v + V_CHUNK, :] = jnp.where(vocab == id_row, 1.0, 0.0).astype(bf16)
        x = mm(et_s[...], oh_s[...])
        gain1, gain2 = wide_gain(g1_s), wide_gain(g2_s)
        a, r1 = norm(x, gain1)
        for f in range(0, 768, F_CHUNK):
            sl = slice(f, f + F_CHUNK)
            p = mm(wgt_s[sl, :], a).astype(bf16).astype(f32)
            q = mm(wut_s[sl, :], a).astype(bf16).astype(f32)
            s = jax.nn.sigmoid(p)
            silu = p * s
            sl_s[sl, :] = silu
            u_s[sl, :] = (silu * q).astype(bf16)
            dp_s[sl, :] = q * s * (1.0 + p * (1.0 - s))
        h = (x + mm(wdt_s[...], u_s[...])).astype(bf16).astype(f32)
        hn, r2 = norm(h, gain2)
        top = jnp.full((1, TILE), -jnp.inf, f32)
        for v in range(0, 2048, V_CHUNK):
            part = mm(e_s[v:v + V_CHUNK, :], hn)
            logit_s[v:v + V_CHUNK, :] = part
            top = jnp.maximum(top, jnp.max(part, axis=0, keepdims=True))
        den = jnp.zeros((1, TILE), f32)
        picked = jnp.zeros((1, TILE), f32)
        for v in range(0, 2048, V_CHUNK):
            part = logit_s[v:v + V_CHUNK, :]
            vocab = lax.broadcasted_iota(jnp.int32, (V_CHUNK, TILE), 0) + v
            picked += jnp.sum(jnp.where(vocab == label_row, part, 0.0), axis=0, keepdims=True)
            part = jnp.exp(part - top)
            den += jnp.sum(part, axis=0, keepdims=True)
            logit_s[v:v + V_CHUNK, :] = part
        loss_out[...] += coef * (top + jnp.log(den) - picked)
        scale = coef / den
        for v in range(0, 2048, V_CHUNK):
            vocab = lax.broadcasted_iota(jnp.int32, (V_CHUNK, TILE), 0) + v
            part = logit_s[v:v + V_CHUNK, :] * scale
            dl_s[v:v + V_CHUNK, :] = (part - jnp.where(vocab == label_row, coef, 0.0)).astype(bf16)
        dhn = mm(et_s[...], dl_s[...])
        dh = norm_back(h, r2, gain2, dhn)
        dhb = dh.astype(bf16)
        dh_s[...] = dh
        for f in range(0, 768, F_CHUNK):
            sl = slice(f, f + F_CHUNK)
            du = mm(wd_s[sl, :], dhb)
            dq_s[sl, :] = (du * sl_s[sl, :]).astype(bf16)
            dpb_s[sl, :] = (du * dp_s[sl, :]).astype(bf16)
            d_wd[sl, :] += mm_nt(u_s[sl, :], dhb)
        d_wg[...] += mm_nt(a, dpb_s[...])
        d_wu[...] += mm_nt(a, dq_s[...])
        da = mm(wg_s[...], dpb_s[...]) + mm(wu_s[...], dq_s[...])
        dx = dh_s[...] + norm_back(x, r1, gain1, da)
        hi = dx.astype(bf16)
        rest = dx - hi.astype(f32)
        mid = rest.astype(bf16)
        low = (rest - mid.astype(f32)).astype(bf16)
        for v in range(0, 2048, V_CHUNK):
            sl = slice(v, v + V_CHUNK)
            oh = oh_s[sl, :]
            d_e[sl, :] += mm_nt(dl_s[sl, :], hn) + mm_nt(oh, hi) + mm_nt(oh, mid) + mm_nt(oh, low)
        return carry

    lax.fori_loop(0, N_TILE, tile_step, 0)

    for half in range(2):
        g_out[:, 16 * half:16 * half + 16, :] = d_e[:, 128 * half:128 * half + 128].reshape(128, 16, 128)
    for base, acc in ((RS_GATE, d_wg), (RS_UP, d_wu), (RS_DOWN, d_wd)):
        n = acc.shape[0]
        per, tiles = n // 128, acc.shape[1] // 128
        for c in range(tiles):
            stage[c * n:(c + 1) * n, :] = acc[:, c * 128:(c + 1) * 128]
            for r in range(per):
                rows[pl.ds(base + r * tiles + c, 128, stride=RS_ROWS), :] = stage[pl.ds(c * n + r, 128, stride=per), :]
    loss = jnp.sum(loss_out[...])
    for r in range(RS_LOSS, RS_ROWS):
        rows[pl.ds(r, 128, stride=RS_ROWS), :] = jnp.full((128, 128), loss, f32)


def local_step(gathered, tok_ids, tok_labels, mask, gain_mlp, gain_head):
    vm = pl.BlockSpec(memory_space=pltpu.VMEM)
    v = lambda dt, *shape: pltpu.VMEM(shape, dt)
    f32, bf16 = jnp.float32, jnp.bfloat16
    tok = lambda t: t.reshape(N_TILE, 1, TILE)
    return pl.pallas_call(
        step_kernel,
        out_shape=(jax.ShapeDtypeStruct((128, RS_ROWS, 128), f32), jax.ShapeDtypeStruct((1, TILE), f32)),
        in_specs=[vm] * 6,
        out_specs=(vm, vm),
        scratch_shapes=[
            v(bf16, 2048, 256), v(bf16, 256, 2048),
            v(bf16, 256, 768), v(bf16, 768, 256), v(bf16, 256, 768), v(bf16, 768, 256), v(bf16, 768, 256), v(bf16, 256, 768),
            v(f32, 256, 128), v(f32, 256, 128),
            v(f32, 2048, 256), v(f32, 256, 768), v(f32, 256, 768), v(f32, 768, 256),
            v(f32, 2048, TILE), v(bf16, 2048, TILE), v(bf16, 2048, TILE),
            v(f32, 768, TILE), v(f32, 768, TILE), v(bf16, 768, TILE), v(f32, 256, TILE), v(bf16, 768, TILE), v(bf16, 768, TILE), v(f32, 1536, 128),
        ],
        compiler_params=pltpu.CompilerParams(vmem_limit_bytes=62 << 20),
        name="local_step",
    )(gathered.reshape(128, AG_ROWS, 128), tok(tok_ids), tok(tok_labels), tok(mask), gain_mlp.reshape(1, 256), gain_head.reshape(1, 256))[0]


def solution(mesh):
    def device_step(tok_ids, tok_labels, loss_mask, table_shard, gain_mlp, gain_head, gate_shard, up_shard, down_shard):
        gathered = gather_all(table_shard, gate_shard, up_shard, down_shard, loss_mask.reshape(32, 128))
        grads = local_step(gathered, tok_ids, tok_labels, loss_mask, gain_mlp, gain_head)
        loss, e_out, wg_out, wu_out, wd_out = reduce_all(grads.reshape(4, 4, 4, 2, RS_ROWS, 128))
        return loss[0, 0], e_out, wg_out, wu_out, wd_out

    row_spec = P("fsdp", None)
    tok_spec = P("fsdp")
    return jax.shard_map(device_step, mesh=mesh, in_specs=(tok_spec, tok_spec, tok_spec, row_spec, P(), P(), row_spec, row_spec, row_spec), out_specs=(P(), row_spec, row_spec, row_spec, row_spec), check_vma=False)
```

time: 1280 us -> 149 us (0.12)
  blocking collectives: 656 us -> 0 us
  waiting for transfers between devices: 332 us -> 0 us
  Pallas kernels: 0 us -> 137 us
  matrix products: 84.6 us -> 0 us
  starting transfers between devices: 82 us -> 0 us
  other arithmetic: 68.1 us -> 0 us
  local copies, waits for them, and re-layouts: 36.1 us -> 9.82 us
  between operations: 14.9 us -> 1.84 us
    unnamed x1 -> x0, blocking collectives: 321 us -> none
    reduce_scatter x1 -> x0, waiting for transfers between devices: 279 us -> none  [scatter_rows(): return lax.psum_scatter(full_rows, 'fsdp', scatter_dimension=0, tiled=True)]
    all_gather x6 -> x0, blocking collectives: 201 us -> none  [gather_rows(): return lax.all_gather(row_shard, 'fsdp', axis=0, tiled=True)]
    pallas_call x0 -> x3, Pallas kernels: none -> 137 us  [the longest x1 74.3 us: local_step(): pl.pallas_call(step_kernel, out_shape=(jax.ShapeDtypeStruct((128, RS_ROWS...]
    psum x2 -> x0, blocking collectives: 134 us -> none  [the longest x1 68.4 us: device_step(): tok_coef = mask_wide / lax.psum(jnp.sum(mask_wide), 'fsdp')]
    dot_general x12 -> x0, matrix products: 84.6 us -> none  [the longest x1 13.3 us: head_forward(): lax.dot_general(h_norm, emb_table, ROW_CONTRACT, preferred_element_type=j...]
    unnamed x33 -> x0, starting transfers between devices: 81.6 us -> none
    all_gather x2 -> x0, waiting for transfers between devices: 51.8 us -> none  [gather_rows(): return lax.all_gather(row_shard, 'fsdp', axis=0, tiled=True)]
  transfers between devices with their start and end apart: 36 -> 0, of which waited for: 2 -> 0; matrix products, arithmetic and copies ran while one was open for 30% -> 0% of each run, Pallas kernels for 0% -> 0%
where the time goes in v1:
time: 149 us
  Pallas kernels  137 us (92%)
  local copies, waits for them, and re-layouts  9.82 us (7%)
  between operations  1.84 us (1%)
    pallas_call x1, Pallas kernels, local_step(): pl.pallas_call(step_kernel, out_shape=(jax.ShapeDtypeStruct((128, RS_ROWS...  74.3 us
    pallas_call x1, Pallas kernels, gather_all(): pl.pallas_call(gather_kernel, out_shape=jax.ShapeDtypeStruct((4, 4, 4, 2,...  31.9 us
    pallas_call x1, Pallas kernels, reduce_all(): pl.pallas_call(reduce_kernel, out_shape=(sds(1, 128), sds(16, 256), sds(2...  31.1 us
    unnamed x18, local copies, waits for them, and re-layouts  9.82 us

profile of v1, /device:TPU:0, one launch (start us, length us, event | category | flops | bytes accessed | tf_op | source)
XLA Modules:
  0.0 148.9 jit_solution(70625002336202149)
XLA Ops:
  0.6 0.0 copy-start.2
  0.6 0.7 copy-done.2
  1.4 0.0 copy-start.3
  1.4 0.7 copy-done.3
  2.0 0.0 copy-start.4
  2.1 0.7 copy-done.4
  2.7 0.0 copy-start.5
  2.7 0.7 copy-done.5
  3.4 0.0 copy-start.6
  3.4 0.7 copy-done.6
  4.1 31.9 %gather_all.1 = bf16[4,4,4,2,96,128]{5,4,3,2,1,0:T(8,128)(2,1)S(1)} custom-call(bf16[16,256]{1,0:T(8,128)(2,1)S(1)} %copy-done.3, bf16[2,768]{1,0:T(2,128)(2,1)S(1)} %copy-done.5, bf16[2,768]{1,0:T(2,128)(2,1)S(1)} %copy-done.6, bf16[6,256]{1,0:T(8,128)(2,1)S(1)} %copy-done.4, s32[32,128]{1,0:T(8,128)S(1)} %bitcast.13), custom_call_target="tpu_custom_call" | custom-call | tf_op jit(solution)/shard_map/gather_all/pallas_call | solution.py:125
  36.0 0.0 copy-start
  36.0 1.6 %copy-done = bf16[4,4,4,2,96,128]{5,4,3,2,1,0:T(8,128)(2,1)} copy-done((bf16[4,4,4,2,96,128]{5,4,3,2,1,0:T(8,128)(2,1)}, bf16[4,4,4,2,96,128]{5,4,3,2,1,0:T(8,128)(2,1)S(1)}, u32[]{:S(2)}) %copy-start) | copy-done | bytes 3145752
  37.6 74.3 %local_step.1 = (f32[128,72,128]{2,1,0:T(8,128)}, f32[1,512]{1,0:T(1,128)}) custom-call(bf16[128,96,128]{2,1,0:T(8,128)(2,1)} %bitcast.10, s32[8,1,512]{2,1,0:T(1,128)} %bitcast.15, s32[8,1,512]{2,1,0:T(1,128)} %bitcast.16, s32[8,1,512]{2,1,0:T(1,128)} %bitcast.12, f32[1,256]{1,0:T(1,128)} %bitcast.17, f32[1,256]{1,0:T(1,128)} %bitcast.18), custom_call_target="tpu_custom_call" | custom-call | tf_op jit(solution)/shard_map/local_step/pallas_call | solution.py:401
  111.9 0.0 copy-start.1
  111.9 2.3 %copy-done.1 = f32[128,72,128]{2,1,0:T(8,128)S(1)} copy-done((f32[128,72,128]{2,1,0:T(8,128)S(1)}, f32[128,72,128]{2,1,0:T(8,128)}, u32[]{:S(2)}) %copy-start.1) | copy-done | bytes 4718616
  114.2 31.1 %reduce_all.1 = (f32[1,128]{1,0:T(1,128)S(1)}, f32[16,256]{1,0:T(8,128)S(1)}, f32[2,768]{1,0:T(2,128)S(1)}, f32[2,768]{1,0:T(2,128)S(1)}, f32[6,256]{1,0:T(8,128)S(1)}) custom-call(f32[4,4,4,2,72,128]{5,4,3,2,1,0:T(8,128)S(1)} %bitcast.11), custom_call_target="tpu_custom_call" | custom-call | tf_op jit(solution)/shard_map/reduce_all/pallas_call | solution.py:246
  145.4 0.6 copy.20
  146.0 0.6 copy.21
  146.6 0.6 copy.22
  147.2 0.6 copy.23
Async XLA Ops:
  0.6 0.7 copy-start.2
  1.4 0.7 copy-start.3
  2.0 0.7 copy-start.4
  2.7 0.7 copy-start.5
  3.4 0.7 copy-start.6
  36.0 1.6 %copy-start = (bf16[4,4,4,2,96,128]{5,4,3,2,1,0:T(8,128)(2,1)}, bf16[4,4,4,2,96,128]{5,4,3,2,1,0:T(8,128)(2,1)S(1)}, u32[]{:S(2)}) copy-start(bf16[4,4,4,2,96,128]{5,4,3,2,1,0:T(8,128)(2,1)S(1)} %gather_all.1) | copy-start | bytes 9437188
  111.9 2.3 %copy-start.1 = (f32[128,72,128]{2,1,0:T(8,128)S(1)}, f32[128,72,128]{2,1,0:T(8,128)}, u32[]{:S(2)}) copy-start(f32[128,72,128]{2,1,0:T(8,128)} %get-tuple-element.11) | copy-start | bytes 14155780

commit v2 on v1

v2 whole, which is shorter than its diff:
```python
import functools

import jax
import jax.numpy as jnp
from jax import lax
from jax.experimental import pallas as pl
from jax.experimental.pallas import tpu as pltpu
from jax.sharding import PartitionSpec as P

NORM_EPS = 1e-6
ROW_CONTRACT = (((1,), (1,)), ((), ()))
MESH = pl.DeviceIdType.MESH
AXIS = "fsdp"
STRIDES = (2, 8, 32)
N_STREAM = 6
AG_ROWS = 96
RS_ROWS = 72
RS_GATE, RS_UP, RS_DOWN, RS_LOSS = 32, 44, 56, 68
RS_STREAMS = ((0, 16), (16, 16), (32, 16), (48, 8), (56, 8), (64, 8))


TILE = 1024
N_TILE = 4096 // TILE
V_CHUNK = 256
F_CHUNK = 256


def torus_partner(v, t):
    near = v + 1 - 2 * lax.rem(v, 2)
    far = 3 - v
    return near + t * (far - near)


def my_place():
    me = lax.axis_index(AXIS)
    core = lax.rem(me, 2)
    coords = (lax.rem(lax.div(me, 2), 4), lax.rem(lax.div(me, 8), 4), lax.div(me, 32))
    return me, core, coords


def greet(me, core, coords):
    barrier = pltpu.get_barrier_semaphore()
    pl.semaphore_signal(barrier, inc=1, device_id=(me + 1 - 2 * core,), device_id_type=MESH)
    for d in range(3):
        for t in range(2):
            other = me + (torus_partner(coords[d], t) - coords[d]) * STRIDES[d]
            pl.semaphore_signal(barrier, inc=1, device_id=(other,), device_id_type=MESH)
    return barrier


def link_of(k, s, core):
    return (k + s) % 3, lax.rem(core + ((k + s) // 3) % 2, 2)


def send_copy(src, dst, send_sem, recv_sem, target):
    return pltpu.make_async_remote_copy(src_ref=src, dst_ref=dst, send_sem=send_sem, recv_sem=recv_sem, device_id=(target,), device_id_type=MESH)


def torus_order(v, t):
    return v + t * (min_int(v, 1) * (lax.rem(v, 3) + 1) - v)


def min_int(a, b):
    return jnp.minimum(a, b)


def first_pairing(k, d, core):
    s = (d - k) % 3
    return link_of(k, s, core)[1]


def gather_send(buf, k, s, me, core, coords, send_sem, recv_sem):
    idx = []
    for d in (2, 1, 0):
        done = len([q for q in range(s) if (k + q) % 3 == d])
        p = torus_order(coords[d], first_pairing(k, d, core))
        idx.append((pl.ds(p, 1), pl.ds(2 * lax.div(p, 2), 2), pl.ds(0, 4))[done])
    d, t = link_of(k, s, core)
    target = me + (torus_partner(coords[d], t) - coords[d]) * STRIDES[d]
    ref = buf.at[(core, k, *idx)]
    return send_copy(ref, ref, send_sem.at[k, s], recv_sem.at[k, s], target)


def gather_phase(me, core, coords, barrier, shards, mask, buf, pack, send_sem, recv_sem, side_send, side_recv):
    cx, cy, cz = coords
    wide = jnp.float32
    e_ref, *w_refs = shards
    pack[0:16, :] = e_ref[:, 0:128].astype(wide)
    pack[16:32, :] = e_ref[:, 128:256].astype(wide)
    pack[32:AG_ROWS, :] = jnp.zeros((AG_ROWS - 32, 128), wide)
    for k, ref in enumerate(w_refs):
        vals = ref[...].astype(wide)
        tiles = vals.shape[1] // 128
        for r in range(vals.shape[0]):
            for c in range(tiles):
                row = 32 + 16 * k + r * tiles + c
                pack[row:row + 1, :] = vals[r:r + 1, c * 128:(c + 1) * 128]
    counts = jnp.zeros((1, 128), wide)
    for i in range(N_TILE):
        row = mask[i].astype(wide)
        for c in range(TILE // 128):
            counts += row[:, c * 128:(c + 1) * 128]
    pack[80:81, :] = counts
    for k in range(N_STREAM):
        pz, py, px = (torus_order(coords[d], first_pairing(k, d, core)) for d in (2, 1, 0))
        buf[core, k, pz, py, px] = pack[16 * k:16 * k + 16, :].astype(jnp.bfloat16)
    pl.semaphore_wait(barrier, 7)
    sent = []
    flight = [None] * N_STREAM
    for s in range(6):
        for k in range(N_STREAM):
            if s > 0:
                flight[k].wait_recv()
            flight[k] = gather_send(buf, k, s, me, core, coords, send_sem, recv_sem)
            flight[k].start()
            sent.append(flight[k])
    for k in range(N_STREAM):
        flight[k].wait_recv()
        ref = buf.at[core, k]
        flight[k] = send_copy(ref, ref, side_send.at[k], side_recv.at[k], me + 1 - 2 * core)
        flight[k].start()
        sent.append(flight[k])
    for c in flight:
        c.wait_recv()
    return sent


def gathered_blocks(k):
    order = ((0, 1, 2, 3), (0, 2, 3, 1))
    for core in range(2):
        first = [(core + ((k + (d - k) % 3) // 3) % 2) % 2 for d in range(3)]
        for z in range(4):
            for y in range(4):
                for x in range(4):
                    yield ((z * 4 + y) * 4 + x) * 2 + core, (core, k, order[first[2]][z], order[first[1]][y], order[first[0]][x])


def recv_shape(k, s):
    sizes = [4, 4, 4]
    for q in range(s + 1):
        sizes[(k + q) % 3] //= 2
    return sizes[2], sizes[1], sizes[0]


def reduce_phase(me, core, coords, g, side, res, recv, send_sem, recv_sem, side_send, side_recv):
    sides = []
    for k, (r0, rn) in enumerate(RS_STREAMS):
        c = send_copy(g.at[:, :, :, 1 - core, pl.ds(r0, rn), :], side.at[:, :, :, pl.ds(r0, rn), :], side_send.at[k], side_recv.at[k], me + 1 - 2 * core)
        c.start()
        sides.append(c)

    def at_dim(d, idx):
        full = [slice(None)] * 3
        full[2 - d] = idx
        return tuple(full)

    pending = {}
    for s in range(7):
        for k, (r0, rn) in enumerate(RS_STREAMS):
            rows = pl.ds(r0, rn)
            if s == 0:
                sides[k].wait_recv()
                side[:, :, :, rows, :] += g[:, :, :, core, rows, :]
                cur = side.at[:, :, :, rows, :]
            else:
                q = s - 1
                for c in pending[k, q]:
                    c.wait_recv()
                d, t = link_of(k, q, core)
                v = coords[d]
                prev = side.at[:, :, :, rows, :] if q == 0 else recv[k * 6 + q - 1]
                cur = recv[k * 6 + q]
                if q < 3:
                    mate = torus_partner(v, 1 - t)
                    lo = jnp.minimum(v, mate)
                    hi = jnp.maximum(v, mate)
                    for j, idx in enumerate((lo, hi)):
                        at = at_dim(d, pl.ds(j, 1))
                        cur[at] += prev[at_dim(d, pl.ds(idx, 1))]
                else:
                    mate = torus_partner(v, t)
                    keep = jnp.where(v > mate, 1, 0)
                    cur[...] += prev[at_dim(d, pl.ds(keep, 1))]
            if s == 6:
                res[rows, :] = cur[0, 0, 0]
                continue
            d, t = link_of(k, s, core)
            v = coords[d]
            mate = torus_partner(v, t)
            target = me + (mate - v) * STRIDES[d]
            dst = recv[k * 6 + s]
            copies = []
            if s < 3:
                far = torus_partner(mate, 1 - t)
                lo = jnp.minimum(mate, far)
                hi = jnp.maximum(mate, far)
                for j, idx in enumerate((lo, hi)):
                    c = send_copy(cur.at[at_dim(d, pl.ds(idx, 1))], dst.at[at_dim(d, pl.ds(j, 1))], send_sem.at[k, 2 * s + j], recv_sem.at[k, 2 * s + j], target)
                    c.start()
                    copies.append(c)
            else:
                give = jnp.where(v > mate, 0, 1)
                c = send_copy(cur.at[at_dim(d, pl.ds(give, 1))], dst, send_sem.at[k, 3 + s], recv_sem.at[k, 3 + s], target)
                c.start()
                copies.append(c)
            pending[k, s] = copies
    return [c for copies in pending.values() for c in copies] + sides


def mm(a, b):
    return jnp.dot(a, b, preferred_element_type=jnp.float32)


def mm_nt(a, b):
    return lax.dot_general(a, b, ROW_CONTRACT, preferred_element_type=jnp.float32)


def compute_scratch():
    v = lambda dt, *shape: pltpu.VMEM(shape, dt)
    f32, bf16 = jnp.float32, jnp.bfloat16
    return [
        v(bf16, 2048, 256), v(bf16, 256, 2048),
        v(bf16, 256, 768), v(bf16, 768, 256), v(bf16, 256, 768), v(bf16, 768, 256), v(bf16, 768, 256), v(bf16, 256, 768),
        v(f32, 256, 128), v(f32, 256, 128), v(f32, 1, TILE),
        v(f32, 2048, 256), v(f32, 256, 768), v(f32, 256, 768), v(f32, 768, 256),
        v(f32, 2048, TILE), v(bf16, 2048, TILE), v(bf16, 2048, TILE),
        v(f32, 768, TILE), v(f32, 768, TILE), v(bf16, 768, TILE), v(f32, 256, TILE), v(bf16, 768, TILE), v(bf16, 768, TILE), v(f32, 1536, 128),
    ]


def compute_phase(buf, ids, labels, mask, g1, g2, g, e_s, et_s, wg_s, wgt_s, wu_s, wut_s, wd_s, wdt_s, g1_s, g2_s, loss_s, d_e, d_wg, d_wu, d_wd, logit_s, dl_s, oh_s, sl_s, dp_s, u_s, dh_s, dq_s, dpb_s, stage):
    f32, bf16 = jnp.float32, jnp.bfloat16
    rows = g.reshape(128 * RS_ROWS, 128)
    for j in range(3):
        for dev, at in gathered_blocks(2 + j):
            rows[dev * RS_ROWS + 16 * j:dev * RS_ROWS + 16 * j + 16, :] = buf[at].astype(f32)
    total = jnp.sum(buf[:, 5, :, :, :, 0:16, :].astype(f32))
    for j, (acc, w, wt) in enumerate(((d_wg, wg_s, wgt_s), (d_wu, wu_s, wut_s), (d_wd, wd_s, wdt_s))):
        n = acc.shape[0]
        per, tiles = n // 128, acc.shape[1] // 128
        for c in range(tiles):
            for r in range(per):
                stage[pl.ds(c * n + r, 128, stride=per), :] = rows[pl.ds(16 * j + r * tiles + c, 128, stride=RS_ROWS), :]
            acc[:, c * 128:(c + 1) * 128] = stage[c * n:(c + 1) * n, :]
        w[...] = acc[...].astype(bf16)
        wt[...] = acc[...].T.astype(bf16)
        acc[...] = jnp.zeros_like(acc)
    for half in range(2):
        for dev, at in gathered_blocks(half):
            e_s[16 * dev:16 * dev + 16, 128 * half:128 * half + 128] = buf[at]
        et_s[128 * half:128 * half + 128, :] = e_s[:, 128 * half:128 * half + 128].T
    g1_s[...] = jnp.broadcast_to(g1[...], (128, 256)).T
    g2_s[...] = jnp.broadcast_to(g2[...], (128, 256)).T
    d_e[...] = jnp.zeros_like(d_e)
    loss_s[...] = jnp.zeros_like(loss_s)

    def wide_gain(ref):
        return jnp.concatenate([ref[...]] * (TILE // 128), axis=1)

    def norm(x, gain):
        r = lax.rsqrt(jnp.mean(x * x, axis=0, keepdims=True) + NORM_EPS)
        return (x * r * gain).astype(bf16), r

    def norm_back(x, r, gain, grad):
        sg = grad * gain
        return r * (sg - x * (r * r) * jnp.mean(sg * x, axis=0, keepdims=True))

    def tile_step(i, carry):
        id_row, label_row = ids[i], labels[i]
        coef = mask[i].astype(f32) / total
        for v in range(0, 2048, V_CHUNK):
            vocab = lax.broadcasted_iota(jnp.int32, (V_CHUNK, TILE), 0) + v
            oh_s[v:v + V_CHUNK, :] = jnp.where(vocab == id_row, 1.0, 0.0).astype(bf16)
        x = mm(et_s[...], oh_s[...])
        gain1, gain2 = wide_gain(g1_s), wide_gain(g2_s)
        a, r1 = norm(x, gain1)
        for f in range(0, 768, F_CHUNK):
            sl = slice(f, f + F_CHUNK)
            p = mm(wgt_s[sl, :], a).astype(bf16).astype(f32)
            q = mm(wut_s[sl, :], a).astype(bf16).astype(f32)
            s = jax.nn.sigmoid(p)
            silu = p * s
            sl_s[sl, :] = silu
            u_s[sl, :] = (silu * q).astype(bf16)
            dp_s[sl, :] = q * s * (1.0 + p * (1.0 - s))
        h = (x + mm(wdt_s[...], u_s[...])).astype(bf16).astype(f32)
        hn, r2 = norm(h, gain2)
        top = jnp.full((1, TILE), -jnp.inf, f32)
        for v in range(0, 2048, V_CHUNK):
            part = mm(e_s[v:v + V_CHUNK, :], hn)
            logit_s[v:v + V_CHUNK, :] = part
            top = jnp.maximum(top, jnp.max(part, axis=0, keepdims=True))
        den = jnp.zeros((1, TILE), f32)
        picked = jnp.zeros((1, TILE), f32)
        for v in range(0, 2048, V_CHUNK):
            part = logit_s[v:v + V_CHUNK, :]
            vocab = lax.broadcasted_iota(jnp.int32, (V_CHUNK, TILE), 0) + v
            picked += jnp.sum(jnp.where(vocab == label_row, part, 0.0), axis=0, keepdims=True)
            part = jnp.exp(part - top)
            den += jnp.sum(part, axis=0, keepdims=True)
            logit_s[v:v + V_CHUNK, :] = part
        loss_s[...] += coef * (top + jnp.log(den) - picked)
        scale = coef / den
        for v in range(0, 2048, V_CHUNK):
            vocab = lax.broadcasted_iota(jnp.int32, (V_CHUNK, TILE), 0) + v
            part = logit_s[v:v + V_CHUNK, :] * scale
            dl_s[v:v + V_CHUNK, :] = (part - jnp.where(vocab == label_row, coef, 0.0)).astype(bf16)
        dhn = mm(et_s[...], dl_s[...])
        dh = norm_back(h, r2, gain2, dhn)
        dhb = dh.astype(bf16)
        dh_s[...] = dh
        for f in range(0, 768, F_CHUNK):
            sl = slice(f, f + F_CHUNK)
            du = mm(wd_s[sl, :], dhb)
            dq_s[sl, :] = (du * sl_s[sl, :]).astype(bf16)
            dpb_s[sl, :] = (du * dp_s[sl, :]).astype(bf16)
            d_wd[sl, :] += mm_nt(u_s[sl, :], dhb)
        d_wg[...] += mm_nt(a, dpb_s[...])
        d_wu[...] += mm_nt(a, dq_s[...])
        da = mm(wg_s[...], dpb_s[...]) + mm(wu_s[...], dq_s[...])
        dx = dh_s[...] + norm_back(x, r1, gain1, da)
        hi = dx.astype(bf16)
        rest = dx - hi.astype(f32)
        mid = rest.astype(bf16)
        low = (rest - mid.astype(f32)).astype(bf16)
        for v in range(0, 2048, V_CHUNK):
            sl = slice(v, v + V_CHUNK)
            oh = oh_s[sl, :]
            d_e[sl, :] += mm_nt(dl_s[sl, :], hn) + mm_nt(oh, hi) + mm_nt(oh, mid) + mm_nt(oh, low)
        return carry

    lax.fori_loop(0, N_TILE, tile_step, 0)

    for half in range(2):
        g[:, :, :, :, 16 * half:16 * half + 16, :] = d_e[:, 128 * half:128 * half + 128].reshape(4, 4, 4, 2, 16, 128)
    for base, acc in ((RS_GATE, d_wg), (RS_UP, d_wu), (RS_DOWN, d_wd)):
        n = acc.shape[0]
        per, tiles = n // 128, acc.shape[1] // 128
        for c in range(tiles):
            stage[c * n:(c + 1) * n, :] = acc[:, c * 128:(c + 1) * 128]
            for r in range(per):
                rows[pl.ds(base + r * tiles + c, 128, stride=RS_ROWS), :] = stage[pl.ds(c * n + r, 128, stride=per), :]
    loss = jnp.sum(loss_s[...])
    for r in range(RS_LOSS, RS_ROWS):
        rows[pl.ds(r, 128, stride=RS_ROWS), :] = jnp.full((128, 128), loss, f32)


def whole_kernel(e_hbm, wg_hbm, wu_hbm, wd_hbm, ids_hbm, labels_hbm, mask_hbm, g1_hbm, g2_hbm, loss_ref, e_out, wg_out, wu_out, wd_out, *refs):
    me, core, coords = my_place()
    barrier = greet(me, core, coords)
    n_in = 9
    local = refs[:n_in]
    in_sem = refs[n_in]
    buf, pack, side, res, g = refs[n_in + 1:n_in + 6]
    recv = refs[n_in + 6:n_in + 42]
    ag_send, ag_recv, ag_side_send, ag_side_recv, rs_send, rs_recv, rs_side_send, rs_side_recv = refs[n_in + 42:n_in + 50]
    scratch = refs[n_in + 50:]
    loads = [pltpu.make_async_copy(src, dst, in_sem.at[i]) for i, (src, dst) in enumerate(zip((e_hbm, wg_hbm, wu_hbm, wd_hbm, ids_hbm, labels_hbm, mask_hbm, g1_hbm, g2_hbm), local))]
    for c in loads:
        c.start()
    for c in loads:
        c.wait()
    e_in, wg_in, wu_in, wd_in, ids, labels, mask, g1, g2 = local
    sent = gather_phase(me, core, coords, barrier, (e_in, wg_in, wu_in, wd_in), mask, buf, pack, ag_send, ag_recv, ag_side_send, ag_side_recv)
    compute_phase(buf, ids, labels, mask, g1, g2, g, *scratch)
    sent += reduce_phase(me, core, coords, g, side, res, recv, rs_send, rs_recv, rs_side_send, rs_side_recv)
    loss_ref[...] = res[RS_LOSS:RS_LOSS + 1, :]
    e_out[:, 0:128] = res[0:16, :]
    e_out[:, 128:256] = res[16:32, :]
    for base, ref in ((RS_GATE, wg_out), (RS_UP, wu_out), (RS_DOWN, wd_out)):
        tiles = ref.shape[1] // 128
        for r in range(ref.shape[0]):
            for c in range(tiles):
                row = base + r * tiles + c
                ref[r:r + 1, c * 128:(c + 1) * 128] = res[row:row + 1, :]
    for c in sent:
        c.wait_send()


def whole_step(*args):
    vm = pl.BlockSpec(memory_space=pltpu.VMEM)
    v = lambda dt, *shape: pltpu.VMEM(shape, dt)
    f32 = jnp.float32
    sds = lambda *shape: jax.ShapeDtypeStruct(shape, f32)
    recvs = [v(f32, *recv_shape(k, s), rn, 128) for k, (_, rn) in enumerate(RS_STREAMS) for s in range(6)]
    sem = pltpu.SemaphoreType.DMA
    return pl.pallas_call(
        whole_kernel,
        out_shape=(sds(1, 128), sds(16, 256), sds(2, 768), sds(2, 768), sds(6, 256)),
        in_specs=[pl.BlockSpec(memory_space=pl.ANY)] * 9,
        out_specs=(vm,) * 5,
        scratch_shapes=[
            *[v(a.dtype, *a.shape) for a in args],
            sem((9,)),
            v(jnp.bfloat16, 2, N_STREAM, 4, 4, 4, 16, 128), v(f32, AG_ROWS, 128),
            v(f32, 4, 4, 4, RS_ROWS, 128), v(f32, RS_ROWS, 128), v(f32, 4, 4, 4, 2, RS_ROWS, 128),
            *recvs,
            sem((N_STREAM, 6)), sem((N_STREAM, 6)), sem((N_STREAM,)), sem((N_STREAM,)),
            sem((N_STREAM, 9)), sem((N_STREAM, 9)), sem((N_STREAM,)), sem((N_STREAM,)),
            *compute_scratch(),
        ],
        compiler_params=pltpu.CompilerParams(collective_id=0, has_side_effects=True, vmem_limit_bytes=62 << 20),
        name="whole_step",
    )(*args)


def solution(mesh):
    def device_step(tok_ids, tok_labels, loss_mask, table_shard, gain_mlp, gain_head, gate_shard, up_shard, down_shard):
        tok = lambda t: t.reshape(N_TILE, 1, TILE)
        loss, e_out, wg_out, wu_out, wd_out = whole_step(table_shard, gate_shard, up_shard, down_shard, tok(tok_ids), tok(tok_labels), tok(loss_mask), gain_mlp.reshape(1, 256), gain_head.reshape(1, 256))
        return loss[0, 0], e_out, wg_out, wu_out, wd_out

    row_spec = P("fsdp", None)
    tok_spec = P("fsdp")
    return jax.shard_map(device_step, mesh=mesh, in_specs=(tok_spec, tok_spec, tok_spec, row_spec, P(), P(), row_spec, row_spec, row_spec), out_specs=(P(), row_spec, row_spec, row_spec, row_spec), check_vma=False)
```

time: 149 us -> 131 us (0.88)
  Pallas kernels: 137 us -> 125 us
  local copies, waits for them, and re-layouts: 9.82 us -> 3.98 us
    pallas_call x3 -> x1, Pallas kernels: 137 us -> 125 us  [whole_step(): pl.pallas_call(whole_kernel, out_shape=(sds(1, 128), sds(16, 256), sds(2,...]
    unnamed x18 -> x12, local copies, waits for them, and re-layouts: 9.82 us -> 3.98 us
where the time goes in v2:
time: 131 us
  Pallas kernels  125 us (95%)
  local copies, waits for them, and re-layouts  3.98 us (3%)
  between operations  1.83 us (1%)
    pallas_call x1, Pallas kernels, whole_step(): pl.pallas_call(whole_kernel, out_shape=(sds(1, 128), sds(16, 256), sds(2,...  125 us
    unnamed x12, local copies, waits for them, and re-layouts  3.98 us

profile of v2, /device:TPU:0, one launch (start us, length us, event | category | flops | bytes accessed | tf_op | source)
XLA Modules:
  0.0 130.8 jit_solution(6484818279389392775)
XLA Ops:
  0.6 125.0 %whole_step.1 = (f32[1,128]{1,0:T(1,128)}, f32[16,256]{1,0:T(8,128)}, f32[2,768]{1,0:T(2,128)}, f32[2,768]{1,0:T(2,128)}, f32[6,256]{1,0:T(8,128)}) custom-call(bf16[16,256]{1,0:T(8,128)(2,1)} %e_hbm.1, bf16[2,768]{1,0:T(2,128)(2,1)} %wg_hbm.1, bf16[2,768]{1,0:T(2,128)(2,1)} %wu_hbm.1, bf16[6,256]{1,0:T(8,128)(2,1)} %wd_hbm.1, s32[4,1,1024]{2,1,0:T(1,128)} %bitcast.7, ...), custom_call_target="tpu_custom_call" | custom-call | tf_op jit(solution)/shard_map/whole_step/pallas_call | solution.py:387
  125.7 0.0 copy-start.3
  125.7 0.7 copy-done.3
  126.4 0.0 copy-start.2
  126.4 1.3 %copy.20 = f32[16,256]{1,0:T(8,128)} copy(f32[16,256]{1,0:T(8,128)} %get-tuple-element.21) | data formatting | bytes 32768
  127.7 0.0 copy-done.2
  127.7 0.0 copy-start.1
  127.7 0.6 copy.21
  128.3 0.1 copy-done.1
  128.4 0.0 copy-start
  128.4 0.6 copy.22
  129.0 0.1 copy-done
  129.1 0.6 copy.23
Async XLA Ops:
  125.7 0.7 copy-start.3
  126.4 1.3 %copy-start.2 = (f32[2,768]{1,0:T(2,128)S(1)}, f32[2,768]{1,0:T(2,128)}, u32[]{:S(2)}) copy-start(f32[2,768]{1,0:T(2,128)} %get-tuple-element.22) | copy-start | bytes 18436
  127.7 0.7 copy-start.1
  128.4 0.7 copy-start

commit v3 on v2

v3 whole, which is shorter than its diff:
```python
import functools

import jax
import jax.numpy as jnp
from jax import lax
from jax.experimental import pallas as pl
from jax.experimental.pallas import tpu as pltpu
from jax.sharding import PartitionSpec as P

NORM_EPS = 1e-6
ROW_CONTRACT = (((1,), (1,)), ((), ()))
MESH = pl.DeviceIdType.MESH
AXIS = "fsdp"
STRIDES = (2, 8, 32)
N_STREAM = 6
AG_ROWS = 96
RS_ROWS = 72
RS_GATE, RS_UP, RS_DOWN, RS_LOSS = 32, 44, 56, 68
RS_STREAMS = tuple((8 * j, 8, j % 6) for j in range(9))
RS_TABLE, RS_WEIGHTS = (0, 1, 2, 3), (4, 5, 6, 7, 8)
N_RS = len(RS_STREAMS)


TILE = 1024
N_TILE = 4096 // TILE
V_CHUNK = 256
F_CHUNK = 384
TG_CHUNK = 1024
EARLY = False


def torus_partner(v, t):
    near = v + 1 - 2 * lax.rem(v, 2)
    far = 3 - v
    return near + t * (far - near)


def my_place():
    me = lax.axis_index(AXIS)
    core = lax.rem(me, 2)
    coords = (lax.rem(lax.div(me, 2), 4), lax.rem(lax.div(me, 8), 4), lax.div(me, 32))
    return me, core, coords


def greet(me, core, coords):
    barrier = pltpu.get_barrier_semaphore()
    pl.semaphore_signal(barrier, inc=1, device_id=(me + 1 - 2 * core,), device_id_type=MESH)
    for d in range(3):
        for t in range(2):
            other = me + (torus_partner(coords[d], t) - coords[d]) * STRIDES[d]
            pl.semaphore_signal(barrier, inc=1, device_id=(other,), device_id_type=MESH)
    return barrier


def link_of(k, s, core):
    return (k + s) % 3, lax.rem(core + ((k + s) // 3) % 2, 2)


def send_copy(src, dst, send_sem, recv_sem, target):
    return pltpu.make_async_remote_copy(src_ref=src, dst_ref=dst, send_sem=send_sem, recv_sem=recv_sem, device_id=(target,), device_id_type=MESH)


def torus_order(v, t):
    return v + t * (min_int(v, 1) * (lax.rem(v, 3) + 1) - v)


def min_int(a, b):
    return jnp.minimum(a, b)


def first_pairing(k, d, core):
    s = (d - k) % 3
    return link_of(k, s, core)[1]


def gather_send(buf, k, s, me, core, coords, send_sem, recv_sem):
    idx = []
    for d in (2, 1, 0):
        done = len([q for q in range(s) if (k + q) % 3 == d])
        p = torus_order(coords[d], first_pairing(k, d, core))
        idx.append((pl.ds(p, 1), pl.ds(2 * lax.div(p, 2), 2), pl.ds(0, 4))[done])
    d, t = link_of(k, s, core)
    target = me + (torus_partner(coords[d], t) - coords[d]) * STRIDES[d]
    ref = buf.at[(core, k, *idx)]
    return send_copy(ref, ref, send_sem.at[k, s], recv_sem.at[k, s], target)


def side_send_half(buf, k, late, me, core, coords, side_send, side_recv):
    d, _ = link_of(k, 5, core)
    p = lax.div(torus_order(coords[d], first_pairing(k, d, core)), 2)
    idx = [pl.ds(0, 4)] * 3
    idx[2 - d] = pl.ds(2 * (p + late * (1 - 2 * p)), 2)
    ref = buf.at[(core, k, *idx)]
    return send_copy(ref, ref, side_send.at[k, late], side_recv.at[k, late], me + 1 - 2 * core)


def gather_phase(me, core, coords, barrier, shards, mask, buf, pack, send_sem, recv_sem, side_send, side_recv):
    cx, cy, cz = coords
    wide = jnp.float32
    e_ref, *w_refs = shards
    pack[0:16, :] = e_ref[:, 0:128].astype(wide)
    pack[16:32, :] = e_ref[:, 128:256].astype(wide)
    pack[32:AG_ROWS, :] = jnp.zeros((AG_ROWS - 32, 128), wide)
    for k, ref in enumerate(w_refs):
        vals = ref[...].astype(wide)
        tiles = vals.shape[1] // 128
        for r in range(vals.shape[0]):
            for c in range(tiles):
                row = 32 + 16 * k + r * tiles + c
                pack[row:row + 1, :] = vals[r:r + 1, c * 128:(c + 1) * 128]
    counts = jnp.zeros((1, 128), wide)
    for i in range(N_TILE):
        row = mask[i].astype(wide)
        for c in range(TILE // 128):
            counts += row[:, c * 128:(c + 1) * 128]
    pack[80:81, :] = counts
    for k in range(N_STREAM):
        pz, py, px = (torus_order(coords[d], first_pairing(k, d, core)) for d in (2, 1, 0))
        buf[core, k, pz, py, px] = pack[16 * k:16 * k + 16, :].astype(jnp.bfloat16)
    pl.semaphore_wait(barrier, 7)
    sent = []
    flight = [None] * N_STREAM
    sides = []
    for s in range(6):
        for k in range(N_STREAM):
            if s > 0:
                flight[k].wait_recv()
            flight[k] = gather_send(buf, k, s, me, core, coords, send_sem, recv_sem)
            flight[k].start()
            sent.append(flight[k])
            if s == 5:
                sides.append(side_send_half(buf, k, 0, me, core, coords, side_send, side_recv))
                sides[-1].start()
    return sent, flight, sides


def gathered_blocks(k):
    order = ((0, 1, 2, 3), (0, 2, 3, 1))
    for core in range(2):
        first = [(core + ((k + (d - k) % 3) // 3) % 2) % 2 for d in range(3)]
        for z in range(4):
            for y in range(4):
                for x in range(4):
                    yield ((z * 4 + y) * 4 + x) * 2 + core, (core, k, order[first[2]][z], order[first[1]][y], order[first[0]][x])


def recv_shape(k, s):
    sizes = [4, 4, 4]
    for q in range(s + 1):
        sizes[(k + q) % 3] //= 2
    return sizes[2], sizes[1], sizes[0]


class Reducer:
    def __init__(self, me, core, coords, g, side, res, recv, send_sem, recv_sem, side_send, side_recv):
        self.me, self.core, self.coords = me, core, coords
        self.g, self.side, self.res, self.recv = g, side, res, recv
        self.sems = (send_sem, recv_sem, side_send, side_recv)
        self.flight = [None] * N_RS
        self.stage = [0] * N_RS
        self.sent = []

    def at_dim(self, d, idx):
        full = [slice(None)] * 3
        full[2 - d] = idx
        return tuple(full)

    def post(self, j, copies):
        for c in copies:
            c.start()
        self.flight[j] = copies
        self.sent += copies

    def advance(self, j):
        me, core, coords = self.me, self.core, self.coords
        send_sem, recv_sem, side_send, side_recv = self.sems
        r0, rn, k = RS_STREAMS[j]
        rows = pl.ds(r0, rn)
        stage = self.stage[j]
        self.stage[j] += 1
        if stage == 0:
            src = self.g.at[:, :, :, 1 - core, rows, :]
            self.post(j, [send_copy(src, self.side.at[:, :, :, rows, :], side_send.at[j], side_recv.at[j], me + 1 - 2 * core)])
            return
        for c in self.flight[j]:
            c.wait_recv()
        if stage == 1:
            self.side[:, :, :, rows, :] += self.g[:, :, :, core, rows, :]
            cur = self.side.at[:, :, :, rows, :]
        else:
            q = stage - 2
            d, t = link_of(k, q, core)
            v = coords[d]
            prev = self.side.at[:, :, :, rows, :] if q == 0 else self.recv[j * 6 + q - 1]
            cur = self.recv[j * 6 + q]
            if q < 3:
                mate = torus_partner(v, 1 - t)
                for i, idx in enumerate((jnp.minimum(v, mate), jnp.maximum(v, mate))):
                    cur[self.at_dim(d, pl.ds(i, 1))] += prev[self.at_dim(d, pl.ds(idx, 1))]
            else:
                mate = torus_partner(v, t)
                keep = jnp.where(v > mate, 1, 0)
                cur[...] += prev[self.at_dim(d, pl.ds(keep, 1))]
        s = stage - 1
        if s == 6:
            self.res[rows, :] = cur[0, 0, 0]
            return
        d, t = link_of(k, s, core)
        v = coords[d]
        mate = torus_partner(v, t)
        target = me + (mate - v) * STRIDES[d]
        dst = self.recv[j * 6 + s]
        if s < 3:
            far = torus_partner(mate, 1 - t)
            copies = [send_copy(cur.at[self.at_dim(d, pl.ds(idx, 1))], dst.at[self.at_dim(d, pl.ds(i, 1))], send_sem.at[j, 2 * s + i], recv_sem.at[j, 2 * s + i], target) for i, idx in enumerate((jnp.minimum(mate, far), jnp.maximum(mate, far)))]
        else:
            give = jnp.where(v > mate, 0, 1)
            copies = [send_copy(cur.at[self.at_dim(d, pl.ds(give, 1))], dst, send_sem.at[j, 3 + s], recv_sem.at[j, 3 + s], target)]
        self.post(j, copies)


def mm(a, b):
    return jnp.dot(a, b, preferred_element_type=jnp.float32)


def mm_nt(a, b):
    return lax.dot_general(a, b, ROW_CONTRACT, preferred_element_type=jnp.float32)


def compute_scratch():
    v = lambda dt, *shape: pltpu.VMEM(shape, dt)
    f32, bf16 = jnp.float32, jnp.bfloat16
    return [
        v(bf16, 2048, 256), v(bf16, 256, 2048),
        v(bf16, 256, 768), v(bf16, 768, 256), v(bf16, 256, 768), v(bf16, 768, 256), v(bf16, 768, 256), v(bf16, 256, 768),
        v(f32, 256, 128), v(f32, 256, 128), v(f32, 1, TILE),
        v(f32, 2048, 256), v(f32, 256, 768), v(f32, 256, 768), v(f32, 768, 256),
        v(f32, 2048, TILE), v(bf16, 2048, TILE), v(bf16, 2048, TILE),
        v(f32, 768, TILE), v(f32, 768, TILE), v(bf16, 768, TILE), v(bf16, 768, TILE), v(bf16, 768, TILE), v(f32, 1536, 128),
        v(f32, 2048, 256), v(bf16, 2048, 128), v(bf16, 256, 2048), v(f32, 8, 2048),
    ]


def compute_phase(buf, ids, labels, mask, g1, g2, g, reducer, ready, e_s, et_s, wg_s, wgt_s, wu_s, wut_s, wd_s, wdt_s, g1_s, g2_s, loss_s, d_e, d_wg, d_wu, d_wd, logit_s, dl_s, oh_s, sl_s, dp_s, u_s, dq_s, dpb_s, stage, s_acc, cnt_s, hn_s, n_s):
    f32, bf16 = jnp.float32, jnp.bfloat16
    g1_s[...] = jnp.broadcast_to(g1[...], (128, 256)).T
    g2_s[...] = jnp.broadcast_to(g2[...], (128, 256)).T
    d_e[...] = jnp.zeros_like(d_e)
    loss_s[...] = jnp.zeros_like(loss_s)
    for half in range(2):
        ready(half)
        for dev, at in gathered_blocks(half):
            e_s[16 * dev:16 * dev + 16, 128 * half:128 * half + 128] = buf[at]
        et_s[128 * half:128 * half + 128, :] = e_s[:, 128 * half:128 * half + 128].T
    s_acc[...] = jnp.zeros_like(s_acc)
    cnt_s[...] = jnp.zeros_like(cnt_s)

    def wide_gain(ref):
        return jnp.concatenate([ref[...]] * (TILE // 128), axis=1)

    def norm(x, gain):
        r = lax.rsqrt(jnp.mean(x * x, axis=0, keepdims=True) + NORM_EPS)
        return (x * r * gain).astype(bf16), r

    def norm_back(x, r, gain, grad):
        sg = grad * gain
        return r * (sg - x * (r * r) * jnp.mean(sg * x, axis=0, keepdims=True))

    def one_hots(i):
        id_row = jnp.where(mask[i] == 1, ids[i], -1)
        label_row = labels[i]
        for v in range(0, 2048, V_CHUNK):
            vocab = lax.broadcasted_iota(jnp.int32, (V_CHUNK, TILE), 0) + v
            oh_s[v:v + V_CHUNK, :] = jnp.where(vocab == id_row, 1.0, 0.0).astype(bf16)
            dl_s[v:v + V_CHUNK, :] = jnp.where(vocab == label_row, 1.0, 0.0).astype(bf16)

    def label_rows(i, carry):
        one_hots(i)
        picked = mm(et_s[...], dl_s[...]).astype(bf16)
        for v in range(0, 2048, TG_CHUNK):
            sl = slice(v, v + TG_CHUNK)
            s_acc[sl, :] += mm_nt(oh_s[sl, :], picked)
        for v in range(0, 2048, V_CHUNK):
            sl = slice(v, v + V_CHUNK)
            count = cnt_s[sl, :]
            for c in range(0, TILE, 128):
                count += oh_s[sl, c:c + 128]
            cnt_s[sl, :] = count
        return carry

    def hidden_rows(i):
        one_hots(i)
        picked = mm(hn_s[...], oh_s[...]).astype(bf16)
        for v in range(0, 2048, TG_CHUNK):
            sl = slice(v, v + TG_CHUNK)
            s_acc[sl, :] += mm_nt(dl_s[sl, :], picked)

    def row_step(j, carry):
        at = pl.ds(pl.multiple_of(j * TILE, TILE), TILE)
        x = et_s[:, at].astype(f32)
        label_sum = s_acc[at, :].T
        n_row = n_s[0:1, at]
        gain1, gain2 = wide_gain(g1_s), wide_gain(g2_s)
        a, r1 = norm(x, gain1)
        for f in range(0, 768, F_CHUNK):
            sl = slice(f, f + F_CHUNK)
            p = mm(wgt_s[sl, :], a).astype(bf16).astype(f32)
            q = mm(wut_s[sl, :], a).astype(bf16).astype(f32)
            s = jax.nn.sigmoid(p)
            silu = p * s
            sl_s[sl, :] = silu
            u_s[sl, :] = (silu * q).astype(bf16)
            dp_s[sl, :] = q * (s + silu * (1.0 - s))
        h = (x + mm(wdt_s[...], u_s[...])).astype(bf16).astype(f32)
        hn, r2 = norm(h, gain2)
        hn_s[:, at] = hn
        top = jnp.full((1, TILE), -jnp.inf, f32)
        for v in range(0, 2048, V_CHUNK):
            part = mm(e_s[v:v + V_CHUNK, :], hn)
            logit_s[v:v + V_CHUNK, :] = part
            top = jnp.maximum(top, jnp.max(part, axis=0, keepdims=True))
        den = jnp.zeros((1, TILE), f32)
        for v in range(0, 2048, V_CHUNK):
            part = jnp.exp(logit_s[v:v + V_CHUNK, :] - top)
            den += jnp.sum(part, axis=0, keepdims=True)
            logit_s[v:v + V_CHUNK, :] = part
        picked = jnp.sum(hn.astype(f32) * label_sum, axis=0, keepdims=True)
        loss_s[...] += coef * (n_row * (top + jnp.log(den)) - picked)
        scale = coef * n_row / den
        for v in range(0, 2048, V_CHUNK):
            dl_s[v:v + V_CHUNK, :] = (logit_s[v:v + V_CHUNK, :] * scale).astype(bf16)
        dhn = mm(et_s[...], dl_s[...]) - coef * label_sum
        dh = norm_back(h, r2, gain2, dhn)
        dhb = dh.astype(bf16)
        for f in range(0, 768, F_CHUNK):
            sl = slice(f, f + F_CHUNK)
            du = mm(wd_s[sl, :], dhb)
            dq_s[sl, :] = (du * sl_s[sl, :]).astype(bf16)
            dpb_s[sl, :] = (du * dp_s[sl, :]).astype(bf16)
            d_wd[sl, :] += mm_nt(u_s[sl, :], dhb)
        d_wg[...] += mm_nt(a, dpb_s[...])
        d_wu[...] += mm_nt(a, dq_s[...])
        da = mm(wg_s[...], dpb_s[...]) + mm(wu_s[...], dq_s[...])
        dx = dh + norm_back(x, r1, gain1, da)
        for v in range(0, 2048, TG_CHUNK):
            sl = slice(v, v + TG_CHUNK)
            d_e[sl, :] += mm_nt(dl_s[sl, :], hn)
        d_e[at, :] += dx.T
        return carry

    lax.fori_loop(0, N_TILE, label_rows, 0)
    n_s[...] = mm_nt(jnp.ones((8, 128), bf16), cnt_s[...])
    rows = g.reshape(128 * RS_ROWS, 128)
    for j in range(3):
        ready(2 + j)
        for dev, at in gathered_blocks(2 + j):
            rows[dev * RS_ROWS + 16 * j:dev * RS_ROWS + 16 * j + 16, :] = buf[at].astype(f32)
    ready(5)
    total = jnp.sum(buf[:, 5, :, :, :, 0:16, :].astype(f32))
    for j, (acc, w, wt) in enumerate(((d_wg, wg_s, wgt_s), (d_wu, wu_s, wut_s), (d_wd, wd_s, wdt_s))):
        n = acc.shape[0]
        per, tiles = n // 128, acc.shape[1] // 128
        for c in range(tiles):
            for r in range(per):
                stage[pl.ds(c * n + r, 128, stride=per), :] = rows[pl.ds(16 * j + r * tiles + c, 128, stride=RS_ROWS), :]
            acc[:, c * 128:(c + 1) * 128] = stage[c * n:(c + 1) * n, :]
        w[...] = acc[...].astype(bf16)
        wt[...] = acc[...].T.astype(bf16)
        acc[...] = jnp.zeros_like(acc)
    coef = 1.0 / total
    lax.fori_loop(0, 2048 // TILE, row_step, 0)

    for base, acc in ((RS_GATE, d_wg), (RS_UP, d_wu), (RS_DOWN, d_wd)):
        n = acc.shape[0]
        per, tiles = n // 128, acc.shape[1] // 128
        for c in range(tiles):
            stage[c * n:(c + 1) * n, :] = acc[:, c * 128:(c + 1) * 128]
            for r in range(per):
                rows[pl.ds(base + r * tiles + c, 128, stride=RS_ROWS), :] = stage[pl.ds(c * n + r, 128, stride=per), :]
    loss = jnp.sum(loss_s[...])
    for r in range(RS_LOSS, RS_ROWS):
        rows[pl.ds(r, 128, stride=RS_ROWS), :] = jnp.full((128, 128), loss, f32)
    s_acc[...] = jnp.zeros_like(s_acc)
    if EARLY:
        for j in RS_WEIGHTS:
            reducer.advance(j)
        for i in range(N_TILE):
            hidden_rows(i)
            for j in RS_WEIGHTS:
                reducer.advance(j)
    else:
        lax.fori_loop(0, N_TILE, lambda i, c: (hidden_rows(i), c)[1], 0)
    for half in range(2):
        cols = slice(128 * half, 128 * half + 128)
        g[:, :, :, :, 16 * half:16 * half + 16, :] = (d_e[:, cols] - coef * s_acc[:, cols]).reshape(4, 4, 4, 2, 16, 128)
    while min(reducer.stage) < 8:
        for j in RS_TABLE + RS_WEIGHTS:
            if reducer.stage[j] < 8:
                reducer.advance(j)


def whole_kernel(*refs):
    me, core, coords = my_place()
    barrier = greet(me, core, coords)
    n_in = 9
    sources, res_out, local, in_sem = refs[:n_in], refs[n_in], refs[n_in + 1:2 * n_in + 1], refs[2 * n_in + 1]
    refs = refs[2 * n_in + 2:]
    buf, pack, side, g = refs[:4]
    recv = refs[4:4 + 6 * N_RS]
    ag_send, ag_recv, ag_side_send, ag_side_recv = refs[4 + 6 * N_RS:8 + 6 * N_RS]
    rs_sems = refs[8 + 6 * N_RS:12 + 6 * N_RS]
    scratch = refs[12 + 6 * N_RS:]
    loads = [pltpu.make_async_copy(src, dst, in_sem.at[i]) for i, (src, dst) in enumerate(zip(sources, local))]
    for c in loads:
        c.start()
    for c in loads:
        c.wait()
    *shards, ids, labels, mask, g1, g2 = local
    sent, flight, sides = gather_phase(me, core, coords, barrier, shards, mask, buf, pack, ag_send, ag_recv, ag_side_send, ag_side_recv)
    late = []
    for k in range(N_STREAM):
        flight[k].wait_recv()
        late.append(side_send_half(buf, k, 1, me, core, coords, ag_side_send, ag_side_recv))
        late[k].start()

    def ready(k):
        sides[k].wait_recv()
        late[k].wait_recv()

    reducer = Reducer(me, core, coords, g, side, res_out, recv, *rs_sems)
    compute_phase(buf, ids, labels, mask, g1, g2, g, reducer, ready, *scratch)
    for c in sent + sides + late + reducer.sent:
        c.wait_send()


def whole_step(*args):
    vm = pl.BlockSpec(memory_space=pltpu.VMEM)
    v = lambda dt, *shape: pltpu.VMEM(shape, dt)
    f32 = jnp.float32
    recvs = [v(f32, *recv_shape(k, s), rn, 128) for _, rn, k in RS_STREAMS for s in range(6)]
    sem = pltpu.SemaphoreType.DMA
    return pl.pallas_call(
        whole_kernel,
        out_shape=jax.ShapeDtypeStruct((RS_ROWS, 128), f32),
        in_specs=[pl.BlockSpec(memory_space=pl.ANY)] * 9,
        out_specs=vm,
        scratch_shapes=[
            *[v(a.dtype, *a.shape) for a in args],
            sem((9,)),
            v(jnp.bfloat16, 2, N_STREAM, 4, 4, 4, 16, 128), v(f32, AG_ROWS, 128),
            v(f32, 4, 4, 4, RS_ROWS, 128), v(f32, 4, 4, 4, 2, RS_ROWS, 128),
            *recvs,
            sem((N_STREAM, 6)), sem((N_STREAM, 6)), sem((N_STREAM, 2)), sem((N_STREAM, 2)),
            sem((N_RS, 9)), sem((N_RS, 9)), sem((N_RS,)), sem((N_RS,)),
            *compute_scratch(),
        ],
        compiler_params=pltpu.CompilerParams(collective_id=0, has_side_effects=True, vmem_limit_bytes=67043328),
        name="whole_step",
    )(*args)


def split_kernel(res, loss_ref, e_out, wg_out, wu_out, wd_out):
    loss_ref[0, 0] = res[RS_LOSS, 0]
    e_out[:, 0:128] = res[0:16, :]
    e_out[:, 128:256] = res[16:32, :]
    for base, ref in ((RS_GATE, wg_out), (RS_UP, wu_out), (RS_DOWN, wd_out)):
        tiles = ref.shape[1] // 128
        for r in range(ref.shape[0]):
            for c in range(tiles):
                row = base + r * tiles + c
                ref[r:r + 1, c * 128:(c + 1) * 128] = res[row:row + 1, :]


def split_result(res):
    vm = pl.BlockSpec(memory_space=pltpu.VMEM)
    sds = lambda *shape: jax.ShapeDtypeStruct(shape, jnp.float32)
    return pl.pallas_call(
        split_kernel,
        out_shape=(sds(1, 1), sds(16, 256), sds(2, 768), sds(2, 768), sds(6, 256)),
        in_specs=[vm],
        out_specs=(pl.BlockSpec(memory_space=pltpu.SMEM), vm, vm, vm, vm),
        compiler_params=pltpu.CompilerParams(vmem_limit_bytes=1 << 20),
        name="split_result",
    )(res)


def solution(mesh):
    def device_step(tok_ids, tok_labels, loss_mask, table_shard, gain_mlp, gain_head, gate_shard, up_shard, down_shard):
        tok = lambda t: t.reshape(N_TILE, 1, TILE)
        loss, e_out, wg_out, wu_out, wd_out = split_result(whole_step(table_shard, gate_shard, up_shard, down_shard, tok(tok_ids), tok(tok_labels), tok(loss_mask), gain_mlp.reshape(1, 256), gain_head.reshape(1, 256)))
        return loss[0, 0], e_out, wg_out, wu_out, wd_out

    row_spec = P("fsdp", None)
    tok_spec = P("fsdp")
    return jax.shard_map(device_step, mesh=mesh, in_specs=(tok_spec, tok_spec, tok_spec, row_spec, P(), P(), row_spec, row_spec, row_spec), out_specs=(P(), row_spec, row_spec, row_spec, row_spec), check_vma=False)
```

time: 131 us -> 108 us (0.82)
  Pallas kernels: 125 us -> 106 us
  local copies, waits for them, and re-layouts: 3.98 us -> 0.76 us
    pallas_call x1 -> x2, Pallas kernels: 125 us -> 106 us  [the longest x1 105 us: whole_step(): pl.pallas_call(whole_kernel, out_shape=jax.ShapeDtypeStruct((RS_ROWS, 128...]
    unnamed x12 -> x2, local copies, waits for them, and re-layouts: 3.98 us -> 0.76 us
where the time goes in v3:
time: 108 us; the launch traced here: 107 us
  Pallas kernels  106 us (98%)
    pallas_call x1, Pallas kernels, whole_step(): pl.pallas_call(whole_kernel, out_shape=jax.ShapeDtypeStruct((RS_ROWS, 128...  105 us

profile of v3, /device:TPU:0, one launch (start us, length us, event | category | flops | bytes accessed | tf_op | source)
XLA Modules:
  0.0 107.3 jit_solution(4241212554319171769)
XLA Ops:
  0.6 105.1 %whole_step.1.res = f32[72,128]{1,0:T(8,128)} custom-call(bf16[16,256]{1,0:T(8,128)(2,1)} %refs_0_.1, bf16[2,768]{1,0:T(2,128)(2,1)} %refs_1_.1, bf16[2,768]{1,0:T(2,128)(2,1)} %refs_2_.1, bf16[6,256]{1,0:T(8,128)(2,1)} %refs_3_.1, s32[4,1,1024]{2,1,0:T(1,128)} %bitcast.6, s32[4,1,1024]{2,1,0:T(1,128)} %bitcast.7, s32[4,1,1024]{2,1,0:T(1,128)} %bitcast.8, ...), custom_call_target="tpu_custom_call" | custom-call | tf_op jit(solution)/shard_map/whole_step/pallas_call | solution.py:442
  105.7 0.0 copy-start
  105.7 0.8 copy-done
  106.5 0.6 split_result.1
Async XLA Ops:
  105.7 0.8 copy-start

commit v4 on v3

--- a/solution.py
+++ b/solution.py
@@ -238,10 +238,11 @@
         v(f32, 2048, TILE), v(bf16, 2048, TILE), v(bf16, 2048, TILE),
         v(f32, 768, TILE), v(f32, 768, TILE), v(bf16, 768, TILE), v(bf16, 768, TILE), v(bf16, 768, TILE), v(f32, 1536, 128),
         v(f32, 2048, 256), v(bf16, 2048, 128), v(bf16, 256, 2048), v(f32, 8, 2048),
+        v(f32, 1024, 256), v(f32, 8, 1024),
     ]
 
 
-def compute_phase(buf, ids, labels, mask, g1, g2, g, reducer, ready, e_s, et_s, wg_s, wgt_s, wu_s, wut_s, wd_s, wdt_s, g1_s, g2_s, loss_s, d_e, d_wg, d_wu, d_wd, logit_s, dl_s, oh_s, sl_s, dp_s, u_s, dq_s, dpb_s, stage, s_acc, cnt_s, hn_s, n_s):
+def compute_phase(buf, ids, labels, mask, g1, g2, g, reducer, ready, core, to_sibling, e_s, et_s, wg_s, wgt_s, wu_s, wut_s, wd_s, wdt_s, g1_s, g2_s, loss_s, d_e, d_wg, d_wu, d_wd, logit_s, dl_s, oh_s, sl_s, dp_s, u_s, dq_s, dpb_s, stage, s_acc, cnt_s, hn_s, n_s, s_in, n_in):
     f32, bf16 = jnp.float32, jnp.bfloat16
     g1_s[...] = jnp.broadcast_to(g1[...], (128, 256)).T
     g2_s[...] = jnp.broadcast_to(g2[...], (128, 256)).T
@@ -249,8 +250,8 @@
     loss_s[...] = jnp.zeros_like(loss_s)
     for half in range(2):
         ready(half)
-        for dev, at in gathered_blocks(half):
-            e_s[16 * dev:16 * dev + 16, 128 * half:128 * half + 128] = buf[at]
+        for dev, place in gathered_blocks(half):
+            e_s[16 * dev:16 * dev + 16, 128 * half:128 * half + 128] = buf[place]
         et_s[128 * half:128 * half + 128, :] = e_s[:, 128 * half:128 * half + 128].T
     s_acc[...] = jnp.zeros_like(s_acc)
     cnt_s[...] = jnp.zeros_like(cnt_s)
@@ -295,8 +296,7 @@
             sl = slice(v, v + TG_CHUNK)
             s_acc[sl, :] += mm_nt(dl_s[sl, :], picked)
 
-    def row_step(j, carry):
-        at = pl.ds(pl.multiple_of(j * TILE, TILE), TILE)
+    def row_step():
         x = et_s[:, at].astype(f32)
         label_sum = s_acc[at, :].T
         n_row = n_s[0:1, at]
@@ -314,6 +314,7 @@
         h = (x + mm(wdt_s[...], u_s[...])).astype(bf16).astype(f32)
         hn, r2 = norm(h, gain2)
         hn_s[:, at] = hn
+        hidden.start()
         top = jnp.full((1, TILE), -jnp.inf, f32)
         for v in range(0, 2048, V_CHUNK):
             part = mm(e_s[v:v + V_CHUNK, :], hn)
@@ -346,15 +347,19 @@
             sl = slice(v, v + TG_CHUNK)
             d_e[sl, :] += mm_nt(dl_s[sl, :], hn)
         d_e[at, :] += dx.T
-        return carry
 
     lax.fori_loop(0, N_TILE, label_rows, 0)
     n_s[...] = mm_nt(jnp.ones((8, 128), bf16), cnt_s[...])
+    at = pl.ds(pl.multiple_of(core * 1024, 1024), 1024)
+    away = pl.ds(pl.multiple_of((1 - core) * 1024, 1024), 1024)
+    sums = [to_sibling(0, s_acc.at[away, :], s_in), to_sibling(1, n_s.at[:, away], n_in)]
+    for c in sums:
+        c.start()
     rows = g.reshape(128 * RS_ROWS, 128)
     for j in range(3):
         ready(2 + j)
-        for dev, at in gathered_blocks(2 + j):
-            rows[dev * RS_ROWS + 16 * j:dev * RS_ROWS + 16 * j + 16, :] = buf[at].astype(f32)
+        for dev, place in gathered_blocks(2 + j):
+            rows[dev * RS_ROWS + 16 * j:dev * RS_ROWS + 16 * j + 16, :] = buf[place].astype(f32)
     ready(5)
     total = jnp.sum(buf[:, 5, :, :, :, 0:16, :].astype(f32))
     for j, (acc, w, wt) in enumerate(((d_wg, wg_s, wgt_s), (d_wu, wu_s, wut_s), (d_wd, wd_s, wdt_s))):
@@ -368,7 +373,12 @@
         wt[...] = acc[...].T.astype(bf16)
         acc[...] = jnp.zeros_like(acc)
     coef = 1.0 / total
-    lax.fori_loop(0, 2048 // TILE, row_step, 0)
+    for c in sums:
+        c.wait_recv()
+    s_acc[at, :] += s_in[...]
+    n_s[:, at] += n_in[...]
+    hidden = to_sibling(2, hn_s.at[:, at], hn_s.at[:, at])
+    row_step()
 
     for base, acc in ((RS_GATE, d_wg), (RS_UP, d_wu), (RS_DOWN, d_wd)):
         n = acc.shape[0]
@@ -380,7 +390,10 @@
     loss = jnp.sum(loss_s[...])
     for r in range(RS_LOSS, RS_ROWS):
         rows[pl.ds(r, 128, stride=RS_ROWS), :] = jnp.full((128, 128), loss, f32)
+    for c in sums:
+        c.wait_send()
     s_acc[...] = jnp.zeros_like(s_acc)
+    hidden.wait()
     if EARLY:
         for j in RS_WEIGHTS:
             reducer.advance(j)
@@ -409,7 +422,8 @@
     recv = refs[4:4 + 6 * N_RS]
     ag_send, ag_recv, ag_side_send, ag_side_recv = refs[4 + 6 * N_RS:8 + 6 * N_RS]
     rs_sems = refs[8 + 6 * N_RS:12 + 6 * N_RS]
-    scratch = refs[12 + 6 * N_RS:]
+    pair_sems = refs[12 + 6 * N_RS:14 + 6 * N_RS]
+    scratch = refs[14 + 6 * N_RS:]
     loads = [pltpu.make_async_copy(src, dst, in_sem.at[i]) for i, (src, dst) in enumerate(zip(sources, local))]
     for c in loads:
         c.start()
@@ -428,7 +442,11 @@
         late[k].wait_recv()
 
     reducer = Reducer(me, core, coords, g, side, res_out, recv, *rs_sems)
-    compute_phase(buf, ids, labels, mask, g1, g2, g, reducer, ready, *scratch)
+
+    def to_sibling(i, src, dst):
+        return send_copy(src, dst, pair_sems[0].at[i], pair_sems[1].at[i], me + 1 - 2 * core)
+
+    compute_phase(buf, ids, labels, mask, g1, g2, g, reducer, ready, core, to_sibling, *scratch)
     for c in sent + sides + late + reducer.sent:
         c.wait_send()
 
@@ -451,7 +469,7 @@
             v(f32, 4, 4, 4, RS_ROWS, 128), v(f32, 4, 4, 4, 2, RS_ROWS, 128),
             *recvs,
             sem((N_STREAM, 6)), sem((N_STREAM, 6)), sem((N_STREAM, 2)), sem((N_STREAM, 2)),
-            sem((N_RS, 9)), sem((N_RS, 9)), sem((N_RS,)), sem((N_RS,)),
+            sem((N_RS, 9)), sem((N_RS, 9)), sem((N_RS,)), sem((N_RS,)), sem((3,)), sem((3,)),
             *compute_scratch(),
         ],
         compiler_params=pltpu.CompilerParams(collective_id=0, has_side_effects=True, vmem_limit_bytes=67043328),

time: 108 us -> 98.1 us (0.908)
  Pallas kernels: 106 us -> 96.2 us
    pallas_call x1, Pallas kernels: 105 us -> 95.6 us  [whole_step(): pl.pallas_call(whole_kernel, out_shape=jax.ShapeDtypeStruct((RS_ROWS, 128...]
where the time goes in v4:
time: 98.1 us; the launch traced here: 97.8 us
  Pallas kernels  96.2 us (98%)
    pallas_call x1, Pallas kernels, whole_step(): pl.pallas_call(whole_kernel, out_shape=jax.ShapeDtypeStruct((RS_ROWS, 128...  95.6 us

profile of v4, /device:TPU:0, one launch (start us, length us, event | category | flops | bytes accessed | tf_op | source)
XLA Modules:
  0.0 97.8 jit_solution(6709934370520591215)
XLA Ops:
  0.6 95.6 %whole_step.1.res = f32[72,128]{1,0:T(8,128)} custom-call(bf16[16,256]{1,0:T(8,128)(2,1)} %refs_0_.1, bf16[2,768]{1,0:T(2,128)(2,1)} %refs_1_.1, bf16[2,768]{1,0:T(2,128)(2,1)} %refs_2_.1, bf16[6,256]{1,0:T(8,128)(2,1)} %refs_3_.1, s32[4,1,1024]{2,1,0:T(1,128)} %bitcast.6, s32[4,1,1024]{2,1,0:T(1,128)} %bitcast.7, s32[4,1,1024]{2,1,0:T(1,128)} %bitcast.8, ...), custom_call_target="tpu_custom_call" | custom-call | tf_op jit(solution)/shard_map/whole_step/pallas_call | solution.py:460
  96.3 0.0 copy-start
  96.3 0.8 copy-done
  97.0 0.6 split_result.1
Async XLA Ops:
  96.3 0.8 copy-start

commit v5 on v4

v5 whole, which is shorter than its diff:
```python
import functools

import jax
import jax.numpy as jnp
from jax import lax
from jax.experimental import pallas as pl
from jax.experimental.pallas import tpu as pltpu
from jax.sharding import PartitionSpec as P

NORM_EPS = 1e-6
ROW_CONTRACT = (((1,), (1,)), ((), ()))
MESH = pl.DeviceIdType.MESH
AXIS = "fsdp"
STRIDES = (2, 8, 32)
N_STREAM = 6
AG_ROWS = 96
RS_ROWS = 72
RS_GATE, RS_UP, RS_DOWN, RS_LOSS = 32, 44, 56, 68
RS_STREAMS = tuple((8 * j, 8, j % 6) for j in range(9))
RS_TABLE, RS_WEIGHTS = (0, 1, 2, 3), (4, 5, 6, 7, 8)
N_RS = len(RS_STREAMS)


TILE = 1024
N_TILE = 4096 // TILE
V_CHUNK = 256
F_CHUNK = 384
TG_CHUNK = 1024


LANES, VOCAB, D_MODEL, D_FF = 128, 2048, 256, 768


def torus_partner(v, t):
    near = v + 1 - 2 * lax.rem(v, 2)
    far = 3 - v
    return near + t * (far - near)


def my_place():
    me = lax.axis_index(AXIS)
    core = lax.rem(me, 2)
    coords = (lax.rem(lax.div(me, 2), 4), lax.rem(lax.div(me, 8), 4), lax.div(me, 32))
    return me, core, coords


def greet(me, core, coords):
    barrier = pltpu.get_barrier_semaphore()
    pl.semaphore_signal(barrier, inc=1, device_id=(me + 1 - 2 * core,), device_id_type=MESH)
    for d in range(3):
        for t in range(2):
            other = me + (torus_partner(coords[d], t) - coords[d]) * STRIDES[d]
            pl.semaphore_signal(barrier, inc=1, device_id=(other,), device_id_type=MESH)
        other = me + (lax.rem(coords[d] + 2, 4) - coords[d]) * STRIDES[d]
        pl.semaphore_signal(barrier, inc=1, device_id=(other,), device_id_type=MESH)
    return barrier


def link_of(k, s, core):
    return (k + s) % 3, lax.rem(core + ((k + s) // 3) % 2, 2)


def send_copy(src, dst, send_sem, recv_sem, target):
    return pltpu.make_async_remote_copy(src_ref=src, dst_ref=dst, send_sem=send_sem, recv_sem=recv_sem, device_id=(target,), device_id_type=MESH)


def torus_order(v, t):
    return v + t * (min_int(v, 1) * (lax.rem(v, 3) + 1) - v)


def min_int(a, b):
    return jnp.minimum(a, b)


def first_pairing(k, d, core):
    return 0 if d == k % 3 else lax.rem(core + k // 3, 2)


def gather_link(k, s, core):
    t = first_pairing(k, (k + 1) % 3, core)
    return (k + 1 + s % 2) % 3, t if s < 2 else 1 - t


def gather_direct(buf, k, me, core, coords, send_sem, recv_sem):
    d = k % 3
    ref = buf.at[(core, k, *(pl.ds(torus_order(coords[e], first_pairing(k, e, core)), 1) for e in (2, 1, 0)))]
    targets = [me + (lax.rem(coords[d] + m, 4) - coords[d]) * STRIDES[d] for m in (1, 2, 3)]
    return [send_copy(ref, ref, send_sem.at[k, i], recv_sem.at[k, i], target) for i, target in enumerate(targets)]


def gather_send(buf, k, s, me, core, coords, send_sem, recv_sem):
    idx = []
    for d in (2, 1, 0):
        if d == k % 3:
            idx.append(pl.ds(0, 4))
            continue
        done = len([q for q in range(s) if (k + 1 + q % 2) % 3 == d])
        p = torus_order(coords[d], first_pairing(k, d, core))
        idx.append((pl.ds(p, 1), pl.ds(2 * lax.div(p, 2), 2), pl.ds(0, 4))[done])
    d, t = gather_link(k, s, core)
    target = me + (torus_partner(coords[d], t) - coords[d]) * STRIDES[d]
    ref = buf.at[(core, k, *idx)]
    return send_copy(ref, ref, send_sem.at[k, 3 + s], recv_sem.at[k, 3 + s], target)


def side_send_half(buf, k, late, me, core, coords, side_send, side_recv):
    d, _ = gather_link(k, 3, core)
    p = lax.div(torus_order(coords[d], first_pairing(k, d, core)), 2)
    idx = [pl.ds(0, 4)] * 3
    idx[2 - d] = pl.ds(2 * (p + late * (1 - 2 * p)), 2)
    ref = buf.at[(core, k, *idx)]
    return send_copy(ref, ref, side_send.at[k, late], side_recv.at[k, late], me + 1 - 2 * core)


def gather_phase(me, core, coords, barrier, early, shards, mask, buf, pack, send_sem, recv_sem, side_send, side_recv):
    cx, cy, cz = coords
    wide = jnp.float32
    e_ref, *w_refs = shards
    pack[0:16, :] = e_ref[:, 0:LANES].astype(wide)
    pack[16:32, :] = e_ref[:, LANES:D_MODEL].astype(wide)
    pack[32:AG_ROWS, :] = jnp.zeros((AG_ROWS - 32, LANES), wide)
    for k, ref in enumerate(w_refs):
        vals = ref[...].astype(wide)
        tiles = vals.shape[1] // LANES
        for r in range(vals.shape[0]):
            for c in range(tiles):
                row = 32 + 16 * k + r * tiles + c
                pack[row:row + 1, :] = vals[r:r + 1, c * LANES:(c + 1) * LANES]
    counts = jnp.zeros((1, LANES), wide)
    for i in range(N_TILE):
        row = mask[i].astype(wide)
        for c in range(TILE // LANES):
            counts += row[:, c * LANES:(c + 1) * LANES]
    pack[80:81, :] = counts
    for k in range(N_STREAM):
        pz, py, px = (torus_order(coords[d], first_pairing(k, d, core)) for d in (2, 1, 0))
        buf[core, k, pz, py, px] = pack[16 * k:16 * k + 16, :].astype(jnp.bfloat16)
    pl.semaphore_wait(barrier, 10)
    sent = []
    flight = []
    sides = []
    for k in range(N_STREAM):
        flight.append(gather_direct(buf, k, me, core, coords, send_sem, recv_sem))
        for c in flight[k]:
            c.start()
    early()
    for s in range(4):
        for k in range(N_STREAM):
            for c in flight[k]:
                c.wait_recv()
            sent += flight[k]
            flight[k] = [gather_send(buf, k, s, me, core, coords, send_sem, recv_sem)]
            flight[k][0].start()
            if s == 3:
                sides.append(side_send_half(buf, k, 0, me, core, coords, side_send, side_recv))
                sides[-1].start()
                sent += flight[k]
    return sent, flight, sides


def gathered_blocks(k):
    order = ((0, 1, 2, 3), (0, 2, 3, 1))
    for core in range(2):
        first = [0 if d == k % 3 else (core + k // 3) % 2 for d in range(3)]
        for z in range(4):
            for y in range(4):
                for x in range(4):
                    yield ((z * 4 + y) * 4 + x) * 2 + core, (core, k, order[first[2]][z], order[first[1]][y], order[first[0]][x])


def recv_shape(k, s):
    sizes = [4, 4, 4]
    for q in range(s + 1):
        sizes[(k + q) % 3] //= 2
    return sizes[2], sizes[1], sizes[0]


class Reducer:
    def __init__(self, me, core, coords, g, side, res, recv, send_sem, recv_sem, side_send, side_recv):
        self.me, self.core, self.coords = me, core, coords
        self.g, self.side, self.res, self.recv = g, side, res, recv
        self.sems = (send_sem, recv_sem, side_send, side_recv)
        self.flight = [None] * N_RS
        self.stage = [0] * N_RS
        self.stay = [None] * N_RS
        self.sent = []

    def at_dim(self, d, idx):
        full = [slice(None)] * 3
        full[2 - d] = idx
        return tuple(full)

    def halves(self, j, core):
        d, t = link_of(RS_STREAMS[j][2], 0, core)
        v = self.coords[d]
        mate = torus_partner(v, t)
        far, near = torus_partner(mate, 1 - t), torus_partner(v, 1 - t)
        return (jnp.minimum(mate, far), jnp.maximum(mate, far)), (jnp.minimum(v, near), jnp.maximum(v, near))

    def cross(self, j, i, idx):
        r0, rn, k = RS_STREAMS[j]
        z, y, x = self.at_dim(k % 3, pl.ds(idx, 1))
        rows = pl.ds(r0, rn)
        return send_copy(self.g.at[z, y, x, 1 - self.core, rows, :], self.side.at[z, y, x, rows, :], self.sems[2].at[j, i], self.sems[3].at[j, i], self.me + 1 - 2 * self.core)

    def start_stay(self):
        for copies in self.stay:
            for c in copies:
                c.start()
            self.sent += copies

    def post(self, j, copies):
        for c in copies:
            c.start()
        self.flight[j] = copies
        self.sent += copies

    def advance(self, j):
        me, core, coords = self.me, self.core, self.coords
        send_sem, recv_sem, side_send, side_recv = self.sems
        r0, rn, k = RS_STREAMS[j]
        rows = pl.ds(r0, rn)
        stage = self.stage[j]
        self.stage[j] += 1
        if stage == 0:
            leave, stay = self.halves(j, 1 - core)
            self.post(j, [self.cross(j, i, idx) for i, idx in enumerate(leave)])
            self.stay[j] = [self.cross(j, 2 + i, idx) for i, idx in enumerate(stay)]
            return
        for c in self.flight[j]:
            c.wait_recv()
        if stage == 1:
            d, _ = link_of(k, 0, core)
            for idx in self.halves(j, core)[0]:
                z, y, x = self.at_dim(d, pl.ds(idx, 1))
                self.side[z, y, x, rows, :] += self.g[z, y, x, core, rows, :]
            cur = self.side.at[:, :, :, rows, :]
        else:
            q = stage - 2
            d, t = link_of(k, q, core)
            v = coords[d]
            prev = self.side.at[:, :, :, rows, :] if q == 0 else self.recv[j * 6 + q - 1]
            cur = self.recv[j * 6 + q]
            if q < 3:
                mate = torus_partner(v, 1 - t)
                if q == 0:
                    for c in self.stay[j]:
                        c.wait_recv()
                for i, idx in enumerate((jnp.minimum(v, mate), jnp.maximum(v, mate))):
                    at = self.at_dim(d, pl.ds(idx, 1))
                    own = prev[at]
                    if q == 0:
                        own += self.g[(*at, core, rows, slice(None))]
                    cur[self.at_dim(d, pl.ds(i, 1))] += own
            else:
                mate = torus_partner(v, t)
                keep = jnp.where(v > mate, 1, 0)
                cur[...] += prev[self.at_dim(d, pl.ds(keep, 1))]
        s = stage - 1
        if s == 6:
            self.res[rows, :] = cur[0, 0, 0]
            return
        d, t = link_of(k, s, core)
        v = coords[d]
        mate = torus_partner(v, t)
        target = me + (mate - v) * STRIDES[d]
        dst = self.recv[j * 6 + s]
        if s < 3:
            far = torus_partner(mate, 1 - t)
            copies = [send_copy(cur.at[self.at_dim(d, pl.ds(idx, 1))], dst.at[self.at_dim(d, pl.ds(i, 1))], send_sem.at[j, 2 * s + i], recv_sem.at[j, 2 * s + i], target) for i, idx in enumerate((jnp.minimum(mate, far), jnp.maximum(mate, far)))]
        else:
            give = jnp.where(v > mate, 0, 1)
            copies = [send_copy(cur.at[self.at_dim(d, pl.ds(give, 1))], dst, send_sem.at[j, 3 + s], recv_sem.at[j, 3 + s], target)]
        self.post(j, copies)


def mm(a, b):
    return jnp.dot(a, b, preferred_element_type=jnp.float32)


def mm_nt(a, b):
    return lax.dot_general(a, b, ROW_CONTRACT, preferred_element_type=jnp.float32)


def compute_scratch():
    v = lambda dt, *shape: pltpu.VMEM(shape, dt)
    f32, bf16 = jnp.float32, jnp.bfloat16
    return [
        v(bf16, VOCAB, D_MODEL), v(bf16, D_MODEL, VOCAB),
        v(bf16, D_MODEL, D_FF), v(bf16, D_FF, D_MODEL), v(bf16, D_MODEL, D_FF), v(bf16, D_FF, D_MODEL), v(bf16, D_FF, D_MODEL), v(bf16, D_MODEL, D_FF),
        v(f32, D_MODEL, LANES), v(f32, D_MODEL, LANES), v(f32, 1, TILE),
        v(f32, VOCAB, D_MODEL), v(f32, D_MODEL, D_FF), v(f32, D_MODEL, D_FF), v(f32, D_FF, D_MODEL),
        v(f32, VOCAB, TILE), v(bf16, VOCAB, TILE), v(bf16, VOCAB, TILE),
        v(f32, D_FF, TILE), v(f32, D_FF, TILE), v(bf16, D_FF, TILE), v(bf16, D_FF, TILE), v(bf16, D_FF, TILE), v(f32, 1536, LANES),
        v(f32, VOCAB, D_MODEL), v(bf16, VOCAB, LANES), v(bf16, D_MODEL, VOCAB), v(f32, 8, VOCAB),
        v(f32, 1024, D_MODEL), v(f32, 8, 1024),
    ]


def early_phase(g1, g2, e_s, et_s, wg_s, wgt_s, wu_s, wut_s, wd_s, wdt_s, g1_s, g2_s, loss_s, d_e, d_wg, d_wu, d_wd, logit_s, dl_s, oh_s, sl_s, dp_s, u_s, dq_s, dpb_s, stage, s_acc, cnt_s, hn_s, n_s, s_in, n_in):
    g1_s[...] = jnp.broadcast_to(g1[...], (LANES, D_MODEL)).T
    g2_s[...] = jnp.broadcast_to(g2[...], (LANES, D_MODEL)).T
    d_e[...] = jnp.zeros_like(d_e)
    loss_s[...] = jnp.zeros_like(loss_s)
    cnt_s[...] = jnp.zeros_like(cnt_s)
    s_acc[...] = jnp.zeros_like(s_acc)


def compute_phase(buf, ids, labels, mask, g1, g2, g, reducer, ready, core, to_sibling, e_s, et_s, wg_s, wgt_s, wu_s, wut_s, wd_s, wdt_s, g1_s, g2_s, loss_s, d_e, d_wg, d_wu, d_wd, logit_s, dl_s, oh_s, sl_s, dp_s, u_s, dq_s, dpb_s, stage, s_acc, cnt_s, hn_s, n_s, s_in, n_in):
    f32, bf16 = jnp.float32, jnp.bfloat16
    for half in range(2):
        ready(half)
        for dev, place in gathered_blocks(half):
            e_s[16 * dev:16 * dev + 16, LANES * half:LANES * half + LANES] = buf[place]
        et_s[LANES * half:LANES * half + LANES, :] = e_s[:, LANES * half:LANES * half + LANES].T

    def wide_gain(ref):
        return jnp.concatenate([ref[...]] * (TILE // LANES), axis=1)

    def norm(x, gain):
        r = lax.rsqrt(jnp.mean(x * x, axis=0, keepdims=True) + NORM_EPS)
        return (x * r * gain).astype(bf16), r

    def norm_back(x, r, gain, grad):
        sg = grad * gain
        return r * (sg - x * (r * r) * jnp.mean(sg * x, axis=0, keepdims=True))

    def one_hots(i):
        id_row = jnp.where(mask[i] == 1, ids[i], -1)
        label_row = labels[i]
        for v in range(0, VOCAB, V_CHUNK):
            vocab = lax.broadcasted_iota(jnp.int32, (V_CHUNK, TILE), 0) + v
            oh_s[v:v + V_CHUNK, :] = jnp.where(vocab == id_row, 1.0, 0.0).astype(bf16)
            dl_s[v:v + V_CHUNK, :] = jnp.where(vocab == label_row, 1.0, 0.0).astype(bf16)

    def label_rows(i, carry):
        one_hots(i)
        picked = mm(et_s[...], dl_s[...]).astype(bf16)
        for v in range(0, VOCAB, TG_CHUNK):
            sl = slice(v, v + TG_CHUNK)
            s_acc[sl, :] += mm_nt(oh_s[sl, :], picked)
        for v in range(0, VOCAB, V_CHUNK):
            sl = slice(v, v + V_CHUNK)
            count = cnt_s[sl, :]
            for c in range(0, TILE, LANES):
                count += oh_s[sl, c:c + LANES]
            cnt_s[sl, :] = count
        return carry

    def hidden_rows(i):
        one_hots(i)
        picked = mm(hn_s[...], oh_s[...]).astype(bf16)
        for v in range(0, VOCAB, TG_CHUNK):
            sl = slice(v, v + TG_CHUNK)
            s_acc[sl, :] += mm_nt(dl_s[sl, :], picked)

    def row_step():
        x = et_s[:, at].astype(f32)
        label_sum = s_acc[at, :].T
        n_row = n_s[0:1, at]
        gain1, gain2 = wide_gain(g1_s), wide_gain(g2_s)
        a, r1 = norm(x, gain1)
        for f in range(0, D_FF, F_CHUNK):
            sl = slice(f, f + F_CHUNK)
            p = mm(wgt_s[sl, :], a).astype(bf16).astype(f32)
            q = mm(wut_s[sl, :], a).astype(bf16).astype(f32)
            s = jax.nn.sigmoid(p)
            silu = p * s
            sl_s[sl, :] = silu
            u_s[sl, :] = (silu * q).astype(bf16)
            dp_s[sl, :] = q * (s + silu * (1.0 - s))
        h = (x + mm(wdt_s[...], u_s[...])).astype(bf16).astype(f32)
        hn, r2 = norm(h, gain2)
        hn_s[:, at] = hn
        hidden.start()
        top = jnp.full((1, TILE), -jnp.inf, f32)
        for v in range(0, VOCAB, V_CHUNK):
            part = mm(e_s[v:v + V_CHUNK, :], hn)
            logit_s[v:v + V_CHUNK, :] = part
            top = jnp.maximum(top, jnp.max(part, axis=0, keepdims=True))
        den = jnp.zeros((1, TILE), f32)
        for v in range(0, VOCAB, V_CHUNK):
            part = jnp.exp(logit_s[v:v + V_CHUNK, :] - top)
            den += jnp.sum(part, axis=0, keepdims=True)
            logit_s[v:v + V_CHUNK, :] = part
        picked = jnp.sum(hn.astype(f32) * label_sum, axis=0, keepdims=True)
        loss_s[...] += coef * (n_row * (top + jnp.log(den)) - picked)
        scale = coef * n_row / den
        for v in range(0, VOCAB, V_CHUNK):
            dl_s[v:v + V_CHUNK, :] = (logit_s[v:v + V_CHUNK, :] * scale).astype(bf16)
        dhn = mm(et_s[...], dl_s[...]) - coef * label_sum
        dh = norm_back(h, r2, gain2, dhn)
        dhb = dh.astype(bf16)
        for f in range(0, D_FF, F_CHUNK):
            sl = slice(f, f + F_CHUNK)
            du = mm(wd_s[sl, :], dhb)
            dq_s[sl, :] = (du * sl_s[sl, :]).astype(bf16)
            dpb_s[sl, :] = (du * dp_s[sl, :]).astype(bf16)
            d_wd[sl, :] += mm_nt(u_s[sl, :], dhb)
        d_wg[...] += mm_nt(a, dpb_s[...])
        d_wu[...] += mm_nt(a, dq_s[...])
        da = mm(wg_s[...], dpb_s[...]) + mm(wu_s[...], dq_s[...])
        dx = dh + norm_back(x, r1, gain1, da)
        for v in range(0, VOCAB, TG_CHUNK):
            sl = slice(v, v + TG_CHUNK)
            d_e[sl, :] += mm_nt(dl_s[sl, :], hn)
        d_e[at, :] += dx.T

    lax.fori_loop(0, N_TILE, label_rows, 0)
    n_s[...] = mm_nt(jnp.ones((8, LANES), bf16), cnt_s[...])
    at = pl.ds(pl.multiple_of(core * 1024, 1024), 1024)
    away = pl.ds(pl.multiple_of((1 - core) * 1024, 1024), 1024)
    sums = [to_sibling(0, s_acc.at[away, :], s_in), to_sibling(1, n_s.at[:, away], n_in)]
    for c in sums:
        c.start()
    rows = g.reshape(LANES * RS_ROWS, LANES)
    for j in range(3):
        ready(2 + j)
        for dev, place in gathered_blocks(2 + j):
            rows[dev * RS_ROWS + 16 * j:dev * RS_ROWS + 16 * j + 16, :] = buf[place].astype(f32)
    ready(5)
    total = jnp.sum(buf[:, 5, :, :, :, 0:16, :].astype(f32))
    for j, (acc, w, wt) in enumerate(((d_wg, wg_s, wgt_s), (d_wu, wu_s, wut_s), (d_wd, wd_s, wdt_s))):
        n = acc.shape[0]
        per, tiles = n // LANES, acc.shape[1] // LANES
        for c in range(tiles):
            for r in range(per):
                stage[pl.ds(c * n + r, LANES, stride=per), :] = rows[pl.ds(16 * j + r * tiles + c, LANES, stride=RS_ROWS), :]
            acc[:, c * LANES:(c + 1) * LANES] = stage[c * n:(c + 1) * n, :]
        w[...] = acc[...].astype(bf16)
        wt[...] = acc[...].T.astype(bf16)
        acc[...] = jnp.zeros_like(acc)
    coef = 1.0 / total
    for c in sums:
        c.wait_recv()
    s_acc[at, :] += s_in[...]
    n_s[:, at] += n_in[...]
    hidden = to_sibling(2, hn_s.at[:, at], hn_s.at[:, at])
    row_step()

    for base, acc in ((RS_GATE, d_wg), (RS_UP, d_wu), (RS_DOWN, d_wd)):
        n = acc.shape[0]
        per, tiles = n // LANES, acc.shape[1] // LANES
        for c in range(tiles):
            stage[c * n:(c + 1) * n, :] = acc[:, c * LANES:(c + 1) * LANES]
            for r in range(per):
                rows[pl.ds(base + r * tiles + c, LANES, stride=RS_ROWS), :] = stage[pl.ds(c * n + r, LANES, stride=per), :]
    loss = jnp.sum(loss_s[...])
    for r in range(RS_LOSS, RS_ROWS):
        rows[pl.ds(r, LANES, stride=RS_ROWS), :] = jnp.full((LANES, LANES), loss, f32)
    for c in sums:
        c.wait_send()
    s_acc[...] = jnp.zeros_like(s_acc)
    hidden.wait()
    lax.fori_loop(0, N_TILE, lambda i, c: (hidden_rows(i), c)[1], 0)
    for half in range(2):
        cols = slice(LANES * half, LANES * half + LANES)
        g[:, :, :, :, 16 * half:16 * half + 16, :] = (d_e[:, cols] - coef * s_acc[:, cols]).reshape(4, 4, 4, 2, 16, LANES)
    for j in RS_TABLE + RS_WEIGHTS:
        reducer.advance(j)
    reducer.start_stay()
    while min(reducer.stage) < 8:
        for j in RS_TABLE + RS_WEIGHTS:
            if reducer.stage[j] < 8:
                reducer.advance(j)


def whole_kernel(*refs):
    me, core, coords = my_place()
    barrier = greet(me, core, coords)
    n_in = 9
    sources, res_out, local, in_sem = refs[:n_in], refs[n_in], refs[n_in + 1:2 * n_in + 1], refs[2 * n_in + 1]
    refs = refs[2 * n_in + 2:]
    buf, pack, side, g = refs[:4]
    recv = refs[4:4 + 6 * N_RS]
    ag_send, ag_recv, ag_side_send, ag_side_recv = refs[4 + 6 * N_RS:8 + 6 * N_RS]
    rs_sems = refs[8 + 6 * N_RS:12 + 6 * N_RS]
    pair_sems = refs[12 + 6 * N_RS:14 + 6 * N_RS]
    scratch = refs[14 + 6 * N_RS:]
    loads = [pltpu.make_async_copy(src, dst, in_sem.at[i]) for i, (src, dst) in enumerate(zip(sources, local))]
    for c in loads:
        c.start()
    for c in loads:
        c.wait()
    *shards, ids, labels, mask, g1, g2 = local
    sent, flight, sides = gather_phase(me, core, coords, barrier, lambda: early_phase(g1, g2, *scratch), shards, mask, buf, pack, ag_send, ag_recv, ag_side_send, ag_side_recv)
    late = []
    for k in range(N_STREAM):
        flight[k][0].wait_recv()
        late.append(side_send_half(buf, k, 1, me, core, coords, ag_side_send, ag_side_recv))
        late[k].start()

    def ready(k):
        sides[k].wait_recv()
        late[k].wait_recv()

    reducer = Reducer(me, core, coords, g, side, res_out, recv, *rs_sems)

    def to_sibling(i, src, dst):
        return send_copy(src, dst, pair_sems[0].at[i], pair_sems[1].at[i], me + 1 - 2 * core)

    compute_phase(buf, ids, labels, mask, g1, g2, g, reducer, ready, core, to_sibling, *scratch)
    for c in sent + sides + late + reducer.sent:
        c.wait_send()


def whole_step(*args):
    vm = pl.BlockSpec(memory_space=pltpu.VMEM)
    v = lambda dt, *shape: pltpu.VMEM(shape, dt)
    f32 = jnp.float32
    recvs = [v(f32, *recv_shape(k, s), rn, LANES) for _, rn, k in RS_STREAMS for s in range(6)]
    sem = pltpu.SemaphoreType.DMA
    return pl.pallas_call(
        whole_kernel,
        out_shape=jax.ShapeDtypeStruct((RS_ROWS, LANES), f32),
        in_specs=[pl.BlockSpec(memory_space=pl.ANY)] * 9,
        out_specs=vm,
        scratch_shapes=[
            *[v(a.dtype, *a.shape) for a in args],
            sem((9,)),
            v(jnp.bfloat16, 2, N_STREAM, 4, 4, 4, 16, LANES), v(f32, AG_ROWS, LANES),
            v(f32, 4, 4, 4, RS_ROWS, LANES), v(f32, 4, 4, 4, 2, RS_ROWS, LANES),
            *recvs,
            sem((N_STREAM, 7)), sem((N_STREAM, 7)), sem((N_STREAM, 2)), sem((N_STREAM, 2)),
            sem((N_RS, 9)), sem((N_RS, 9)), sem((N_RS, 4)), sem((N_RS, 4)), sem((3,)), sem((3,)),
            *compute_scratch(),
        ],
        compiler_params=pltpu.CompilerParams(collective_id=0, has_side_effects=True, vmem_limit_bytes=67043328),
        name="whole_step",
    )(*args)


def split_kernel(res, loss_ref, e_out, wg_out, wu_out, wd_out):
    loss_ref[0, 0] = res[RS_LOSS, 0]
    e_out[:, 0:LANES] = res[0:16, :]
    e_out[:, LANES:D_MODEL] = res[16:32, :]
    for base, ref in ((RS_GATE, wg_out), (RS_UP, wu_out), (RS_DOWN, wd_out)):
        tiles = ref.shape[1] // LANES
        for r in range(ref.shape[0]):
            for c in range(tiles):
                row = base + r * tiles + c
                ref[r:r + 1, c * LANES:(c + 1) * LANES] = res[row:row + 1, :]


def split_result(res):
    vm = pl.BlockSpec(memory_space=pltpu.VMEM)
    sds = lambda *shape: jax.ShapeDtypeStruct(shape, jnp.float32)
    return pl.pallas_call(
        split_kernel,
        out_shape=(sds(1, 1), sds(16, D_MODEL), sds(2, D_FF), sds(2, D_FF), sds(6, D_MODEL)),
        in_specs=[vm],
        out_specs=(pl.BlockSpec(memory_space=pltpu.SMEM), vm, vm, vm, vm),
        compiler_params=pltpu.CompilerParams(vmem_limit_bytes=1 << 20),
        name="split_result",
    )(res)


def solution(mesh):
    def device_step(tok_ids, tok_labels, loss_mask, table_shard, gain_mlp, gain_head, gate_shard, up_shard, down_shard):
        tok = lambda t: t.reshape(N_TILE, 1, TILE)
        loss, e_out, wg_out, wu_out, wd_out = split_result(whole_step(table_shard, gate_shard, up_shard, down_shard, tok(tok_ids), tok(tok_labels), tok(loss_mask), gain_mlp.reshape(1, D_MODEL), gain_head.reshape(1, D_MODEL)))
        return loss[0, 0], e_out, wg_out, wu_out, wd_out

    row_spec = P("fsdp", None)
    tok_spec = P("fsdp")
    return jax.shard_map(device_step, mesh=mesh, in_specs=(tok_spec, tok_spec, tok_spec, row_spec, P(), P(), row_spec, row_spec, row_spec), out_specs=(P(), row_spec, row_spec, row_spec, row_spec), check_vma=False)
```

time: 98.1 us -> 94.8 us (0.966)
  Pallas kernels: 96.2 us -> 93 us
    pallas_call x2, Pallas kernels: 96.2 us -> 93 us  [the longest x1 92.4 us: whole_step(): pl.pallas_call(whole_kernel, out_shape=jax.ShapeDtypeStruct((RS_ROWS, LAN...]
where the time goes in v5:
time: 94.8 us; the launch traced here: 94.6 us
  Pallas kernels  93 us (98%)
    pallas_call x1, Pallas kernels, whole_step(): pl.pallas_call(whole_kernel, out_shape=jax.ShapeDtypeStruct((RS_ROWS, LAN...  92.4 us

profile of v5, /device:TPU:0, one launch (start us, length us, event | category | flops | bytes accessed | tf_op | source)
XLA Modules:
  0.0 94.6 jit_solution(536037271984767934)
XLA Ops:
  0.6 92.4 %whole_step.1.res = f32[72,128]{1,0:T(8,128)} custom-call(bf16[16,256]{1,0:T(8,128)(2,1)} %refs_0_.1, bf16[2,768]{1,0:T(2,128)(2,1)} %refs_1_.1, bf16[2,768]{1,0:T(2,128)(2,1)} %refs_2_.1, bf16[6,256]{1,0:T(8,128)(2,1)} %refs_3_.1, s32[4,1,1024]{2,1,0:T(1,128)} %bitcast.6, s32[4,1,1024]{2,1,0:T(1,128)} %bitcast.7, s32[4,1,1024]{2,1,0:T(1,128)} %bitcast.8, ...), custom_call_target="tpu_custom_call" | custom-call | tf_op jit(solution)/shard_map/whole_step/pallas_call | solution.py:513
  93.0 0.0 copy-start
  93.0 0.8 copy-done
  93.8 0.6 split_result.1
Async XLA Ops:
  93.0 0.8 copy-start

commit v6 on v5

--- a/solution.py
+++ b/solution.py
@@ -306,12 +306,14 @@
     s_acc[...] = jnp.zeros_like(s_acc)
 
 
-def compute_phase(buf, ids, labels, mask, g1, g2, g, reducer, ready, core, to_sibling, e_s, et_s, wg_s, wgt_s, wu_s, wut_s, wd_s, wdt_s, g1_s, g2_s, loss_s, d_e, d_wg, d_wu, d_wd, logit_s, dl_s, oh_s, sl_s, dp_s, u_s, dq_s, dpb_s, stage, s_acc, cnt_s, hn_s, n_s, s_in, n_in):
+def compute_phase(buf, ids, labels, mask, g1, g2, g, reducer, ready, forward, core, to_sibling, e_s, et_s, wg_s, wgt_s, wu_s, wut_s, wd_s, wdt_s, g1_s, g2_s, loss_s, d_e, d_wg, d_wu, d_wd, logit_s, dl_s, oh_s, sl_s, dp_s, u_s, dq_s, dpb_s, stage, s_acc, cnt_s, hn_s, n_s, s_in, n_in):
     f32, bf16 = jnp.float32, jnp.bfloat16
     for half in range(2):
         ready(half)
         for dev, place in gathered_blocks(half):
             e_s[16 * dev:16 * dev + 16, LANES * half:LANES * half + LANES] = buf[place]
+        if half == 1:
+            forward(range(2, N_STREAM))
         et_s[LANES * half:LANES * half + LANES, :] = e_s[:, LANES * half:LANES * half + LANES].T
 
     def wide_gain(ref):
@@ -485,10 +487,14 @@
     *shards, ids, labels, mask, g1, g2 = local
     sent, flight, sides = gather_phase(me, core, coords, barrier, lambda: early_phase(g1, g2, *scratch), shards, mask, buf, pack, ag_send, ag_recv, ag_side_send, ag_side_recv)
     late = []
-    for k in range(N_STREAM):
-        flight[k][0].wait_recv()
-        late.append(side_send_half(buf, k, 1, me, core, coords, ag_side_send, ag_side_recv))
-        late[k].start()
+
+    def forward(streams):
+        for k in streams:
+            flight[k][0].wait_recv()
+            late.append(side_send_half(buf, k, 1, me, core, coords, ag_side_send, ag_side_recv))
+            late[k].start()
+
+    forward(range(2))
 
     def ready(k):
         sides[k].wait_recv()
@@ -499,7 +505,7 @@
     def to_sibling(i, src, dst):
         return send_copy(src, dst, pair_sems[0].at[i], pair_sems[1].at[i], me + 1 - 2 * core)
 
-    compute_phase(buf, ids, labels, mask, g1, g2, g, reducer, ready, core, to_sibling, *scratch)
+    compute_phase(buf, ids, labels, mask, g1, g2, g, reducer, ready, forward, core, to_sibling, *scratch)
     for c in sent + sides + late + reducer.sent:
         c.wait_send()
 

time: 94.8 us -> 94.8 us (level)
  no operation moved by 1% of the time
where the time goes in v6:
time: 94.8 us; the launch traced here: 94.5 us
  Pallas kernels  92.9 us (98%)
    pallas_call x1, Pallas kernels, whole_step(): pl.pallas_call(whole_kernel, out_shape=jax.ShapeDtypeStruct((RS_ROWS, LAN...  92.3 us

profile of v6, /device:TPU:0, one launch (start us, length us, event | category | flops | bytes accessed | tf_op | source)
XLA Modules:
  0.0 94.5 jit_solution(16662950951064930557)
XLA Ops:
  0.6 92.3 %whole_step.1.res = f32[72,128]{1,0:T(8,128)} custom-call(bf16[16,256]{1,0:T(8,128)(2,1)} %refs_0_.1, bf16[2,768]{1,0:T(2,128)(2,1)} %refs_1_.1, bf16[2,768]{1,0:T(2,128)(2,1)} %refs_2_.1, bf16[6,256]{1,0:T(8,128)(2,1)} %refs_3_.1, s32[4,1,1024]{2,1,0:T(1,128)} %bitcast.6, s32[4,1,1024]{2,1,0:T(1,128)} %bitcast.7, s32[4,1,1024]{2,1,0:T(1,128)} %bitcast.8, ...), custom_call_target="tpu_custom_call" | custom-call | tf_op jit(solution)/shard_map/whole_step/pallas_call | solution.py:519
  93.0 0.0 copy-start
  93.0 0.8 copy-done
  93.7 0.6 split_result.1
Async XLA Ops:
  93.0 0.8 copy-start
